TPU v7x, 16 devices: a whole 2x2x2 slice. The times are simulated.
16 devices in a mesh: tp: 2 (over z), dp: 8 (over y, x, core).
Axes of the slice: x: 2, y: 2, z: 2, core: 2. Of those that a mesh axis runs over, the one named last changes fastest.
Arguments:
- tokens: int32 [16, 1024], P('dp')
- labels: int32 [16, 1024], P('dp')
- embedding: float32 [50304, 512], P('tp')
- vec_params: float32 [16, 512], replicated
- w_qkv: float32 [2, 512, 1536], P(None, None, 'tp')
- b_qkv: float32 [2, 8, 192], P(None, 'tp')
- w_out: float32 [2, 512, 512], P(None, 'tp')
- w_up: float32 [2, 512, 2048], P(None, None, 'tp')
- b_up: float32 [2, 2048], P(None, 'tp')
- w_down: float32 [2, 2048, 512], P(None, 'tp')
- mom_embedding: float32 [50304, 512], P('tp')
- mom_vec_params: float32 [16, 512], replicated
- mom_w_qkv: float32 [2, 512, 1536], P(None, None, 'tp')
- mom_b_qkv: float32 [2, 8, 192], P(None, 'tp')
- mom_w_out: float32 [2, 512, 512], P(None, 'tp')
- mom_w_up: float32 [2, 512, 2048], P(None, None, 'tp')
- mom_b_up: float32 [2, 2048], P(None, 'tp')
- mom_w_down: float32 [2, 2048, 512], P(None, 'tp')
- vel_embedding: float32 [50304, 512], P('tp')
- vel_vec_params: float32 [16, 512], replicated
- vel_w_qkv: float32 [2, 512, 1536], P(None, None, 'tp')
- vel_b_qkv: float32 [2, 8, 192], P(None, 'tp')
- vel_w_out: float32 [2, 512, 512], P(None, 'tp')
- vel_w_up: float32 [2, 512, 2048], P(None, None, 'tp')
- vel_b_up: float32 [2, 2048], P(None, 'tp')
- vel_w_down: float32 [2, 2048, 512], P(None, 'tp')
Outputs:
- output 1: float32 [], replicated
- output 2: float32 [50304, 512], P('tp')
- output 3: float32 [16, 512], replicated
- output 4: float32 [2, 512, 1536], P(None, None, 'tp')
- output 5: float32 [2, 8, 192], P(None, 'tp')
- output 6: float32 [2, 512, 512], P(None, 'tp')
- output 7: float32 [2, 512, 2048], P(None, None, 'tp')
- output 8: float32 [2, 2048], P(None, 'tp')
- output 9: float32 [2, 2048, 512], P(None, 'tp')
- output 10: float32 [50304, 512], P('tp')
- output 11: float32 [16, 512], replicated
- output 12: float32 [2, 512, 1536], P(None, None, 'tp')
- output 13: float32 [2, 8, 192], P(None, 'tp')
- output 14: float32 [2, 512, 512], P(None, 'tp')
- output 15: float32 [2, 512, 2048], P(None, None, 'tp')
- output 16: float32 [2, 2048], P(None, 'tp')
- output 17: float32 [2, 2048, 512], P(None, 'tp')
- output 18: float32 [50304, 512], P('tp')
- output 19: float32 [16, 512], replicated
- output 20: float32 [2, 512, 1536], P(None, None, 'tp')
- output 21: float32 [2, 8, 192], P(None, 'tp')
- output 22: float32 [2, 512, 512], P(None, 'tp')
- output 23: float32 [2, 512, 2048], P(None, None, 'tp')
- output 24: float32 [2, 2048], P(None, 'tp')
- output 25: float32 [2, 2048, 512], P(None, 'tp')
- output 26: bfloat16 [50304, 512], P('tp')
- output 27: bfloat16 [16, 512], replicated
- output 28: bfloat16 [2, 512, 1536], P(None, None, 'tp')
- output 29: bfloat16 [2, 8, 192], P(None, 'tp')
- output 30: bfloat16 [2, 512, 512], P(None, 'tp')
- output 31: bfloat16 [2, 512, 2048], P(None, None, 'tp')
- output 32: bfloat16 [2, 2048], P(None, 'tp')
- output 33: bfloat16 [2, 2048, 512], P(None, 'tp')
All inputs are finite; a program needn't handle non-finite values.
Results may differ from a plain program's by a relative error of at most 0.001.
Values sent between devices are 32-bit elements.
A program may use at most 1.75 GiB of HBM per device.

v0:
```python
import math
import jax
import jax.numpy as jnp
from jax import lax
from jax.sharding import PartitionSpec as P

LN_EPS = 1e-5
CLIP_NORM = 1.0
BETA_ONE = 0.9
BETA_TWO = 0.95
ADAM_EPS = 1e-8
WEIGHT_DECAY = 0.1
LEARN_RATE = 1e-3
STEP_COUNT = 10
DECAYED = (True, False, True, False, True, True, False, True)
PARAM_SPECS = (P('tp', None), P(None, None), P(None, None, 'tp'), P(None, 'tp', None), P(None, 'tp', None), P(None, None, 'tp'), P(None, 'tp'), P(None, 'tp', None))
CONTRACT_ROWS = (((0,), (0,)), ((), ()))
CONTRACT_COLS = (((1,), (1,)), ((), ()))


def alibi_slopes(heads):
    closest = 2 ** int(math.floor(math.log2(heads)))
    first_base = 2.0 ** (-8.0 / closest)
    slopes = [first_base ** (head_idx + 1) for head_idx in range(closest)]
    extra_base = 2.0 ** (-4.0 / closest)
    extra_count = min(closest, heads - closest)
    return slopes + [extra_base ** (2 * head_idx + 1) for head_idx in range(extra_count)]


def layer_norm(values, gain, bias):
    centred = values - jnp.mean(values, axis=-1, keepdims=True)
    variance = jnp.mean(centred * centred, axis=-1, keepdims=True)
    return centred * lax.rsqrt(variance + LN_EPS) * gain + bias


def gelu_tanh(values):
    return jax.nn.gelu(values, approximate=True)


def attn_probs(query, key_blk, slopes, scale):
    seq_len = query.shape[1]
    positions = jnp.arange(seq_len)
    rel_pos = (positions[None, :] - positions[:, None]).astype(jnp.float32)
    causal = positions[None, :] <= positions[:, None]
    scores = jnp.einsum('bqhd,bkhd->bhqk', query, key_blk, preferred_element_type=jnp.float32) * scale
    scores = scores + slopes[None, :, None, None] * rel_pos[None, None]
    scores = jnp.where(causal[None, None], scores, -jnp.inf)
    return jax.nn.softmax(scores, axis=-1)


def adam_update(master, grad_arr, moment, velocity, decayed):
    mom_new = BETA_ONE * moment + (1.0 - BETA_ONE) * grad_arr
    vel_new = BETA_TWO * velocity + (1.0 - BETA_TWO) * grad_arr * grad_arr
    mom_hat = mom_new / (1.0 - BETA_ONE ** STEP_COUNT)
    vel_hat = vel_new / (1.0 - BETA_TWO ** STEP_COUNT)
    direction = mom_hat / (jnp.sqrt(vel_hat) + ADAM_EPS)
    if decayed:
        direction = direction + WEIGHT_DECAY * master
    return master - LEARN_RATE * direction, mom_new, vel_new


def local_grads(tokens, labels, masters, tp_size, dp_size):
    embedding, vec_params, w_qkv, b_qkv, w_out, w_up, b_up, w_down = masters
    tp_rank = lax.axis_index('tp')
    vocab_loc = embedding.shape[0]
    batch_loc, seq_len = tokens.shape
    n_tok = batch_loc * seq_len
    n_total = n_tok * dp_size
    layers = w_qkv.shape[0]
    heads_loc = b_qkv.shape[1]
    head_dim = b_qkv.shape[2] // 3
    scale = head_dim ** -0.5
    slope_all = jnp.array(alibi_slopes(heads_loc * tp_size), dtype=jnp.float32)
    slope_loc = lax.dynamic_slice_in_dim(slope_all, tp_rank * heads_loc, heads_loc)
    emb_b = embedding.astype(jnp.bfloat16)
    wqkv_b = w_qkv.astype(jnp.bfloat16)
    wout_b = w_out.astype(jnp.bfloat16)
    wup_b = w_up.astype(jnp.bfloat16)
    wdown_b = w_down.astype(jnp.bfloat16)

    id_local = tokens.reshape(-1) - tp_rank * vocab_loc
    in_shard = (id_local >= 0) & (id_local < vocab_loc)
    safe_ids = jnp.clip(id_local, 0, vocab_loc - 1)
    picked = jnp.take(emb_b, safe_ids, axis=0)
    x_embed = lax.psum(jnp.where(in_shard[:, None], picked.astype(jnp.float32), 0.0), 'tp')
    resid, ln_zero_vjp = jax.vjp(layer_norm, x_embed, vec_params[0], vec_params[1])

    saved = []
    for layer in range(layers):
        row_base = 2 + 6 * layer
        normed_one, ln_one_vjp = jax.vjp(layer_norm, resid, vec_params[row_base], vec_params[row_base + 1])
        act_in = normed_one.astype(jnp.bfloat16)
        qkv = (jnp.dot(act_in, wqkv_b[layer], preferred_element_type=jnp.float32) + b_qkv[layer].reshape(-1)).astype(jnp.bfloat16)
        qkv = qkv.reshape(batch_loc, seq_len, heads_loc, 3, head_dim)
        query = qkv[:, :, :, 0]
        key_blk = qkv[:, :, :, 1]
        value_blk = qkv[:, :, :, 2]
        probs = attn_probs(query, key_blk, slope_loc, scale)
        context = jnp.einsum('bhqk,bkhd->bqhd', probs.astype(jnp.bfloat16), value_blk, preferred_element_type=jnp.float32).astype(jnp.bfloat16).reshape(n_tok, heads_loc * head_dim)
        attn_out = lax.psum(jnp.dot(context, wout_b[layer], preferred_element_type=jnp.float32), 'tp') + vec_params[row_base + 2]
        mid = resid + attn_out
        normed_two, ln_two_vjp = jax.vjp(layer_norm, mid, vec_params[row_base + 3], vec_params[row_base + 4])
        mlp_in = normed_two.astype(jnp.bfloat16)
        pre_act = jnp.dot(mlp_in, wup_b[layer], preferred_element_type=jnp.float32) + b_up[layer]
        act_out, gelu_vjp = jax.vjp(gelu_tanh, pre_act)
        hidden = act_out.astype(jnp.bfloat16)
        resid = mid + lax.psum(jnp.dot(hidden, wdown_b[layer], preferred_element_type=jnp.float32), 'tp') + vec_params[row_base + 5]
        saved.append((ln_one_vjp, act_in, query, key_blk, value_blk, context, ln_two_vjp, mlp_in, gelu_vjp, hidden))

    final_row = 2 + 6 * layers
    normed_fin, ln_fin_vjp = jax.vjp(layer_norm, resid, vec_params[final_row], vec_params[final_row + 1])
    head_in = normed_fin.astype(jnp.bfloat16)
    logits = lax.dot_general(head_in, emb_b, CONTRACT_COLS, preferred_element_type=jnp.float32)
    glob_max = lax.pmax(jnp.max(logits, axis=1), 'tp')
    shifted = jnp.exp(logits - glob_max[:, None])
    sum_exp = lax.psum(jnp.sum(shifted, axis=1), 'tp')
    lab_local = labels.reshape(-1) - tp_rank * vocab_loc
    onehot = jnp.arange(vocab_loc)[None, :] == lab_local[:, None]
    target = lax.psum(jnp.sum(jnp.where(onehot, logits, 0.0), axis=1), 'tp')
    loss_sum = jnp.sum(glob_max + jnp.log(sum_exp) - target)

    d_logits = ((shifted / sum_exp[:, None] - onehot.astype(jnp.float32)) / n_total).astype(jnp.bfloat16)
    g_emb = lax.dot_general(d_logits, head_in, CONTRACT_ROWS, preferred_element_type=jnp.float32)
    d_head = lax.psum(jnp.dot(d_logits, emb_b, preferred_element_type=jnp.float32), 'tp')
    vec_grads = {}
    d_resid, vec_grads[final_row], vec_grads[final_row + 1] = ln_fin_vjp(d_head)
    g_qkv_all = {}
    g_bqkv_all = {}
    g_out_all = {}
    g_up_all = {}
    g_bup_all = {}
    g_down_all = {}
    for layer in reversed(range(layers)):
        ln_one_vjp, act_in, query, key_blk, value_blk, context, ln_two_vjp, mlp_in, gelu_vjp, hidden = saved[layer]
        row_base = 2 + 6 * layer
        vec_grads[row_base + 5] = jnp.sum(d_resid, axis=0)
        d_out = d_resid.astype(jnp.bfloat16)
        g_down_all[layer] = lax.dot_general(hidden, d_out, CONTRACT_ROWS, preferred_element_type=jnp.float32)
        d_hidden = lax.dot_general(d_out, wdown_b[layer], CONTRACT_COLS, preferred_element_type=jnp.float32)
        d_pre = gelu_vjp(d_hidden)[0]
        g_bup_all[layer] = jnp.sum(d_pre, axis=0)
        d_pre_b = d_pre.astype(jnp.bfloat16)
        g_up_all[layer] = lax.dot_general(mlp_in, d_pre_b, CONTRACT_ROWS, preferred_element_type=jnp.float32)
        d_norm_two = lax.psum(lax.dot_general(d_pre_b, wup_b[layer], CONTRACT_COLS, preferred_element_type=jnp.float32), 'tp')
        d_mid_ln, vec_grads[row_base + 3], vec_grads[row_base + 4] = ln_two_vjp(d_norm_two)
        d_mid = d_resid + d_mid_ln
        vec_grads[row_base + 2] = jnp.sum(d_mid, axis=0)
        d_attn = d_mid.astype(jnp.bfloat16)
        g_out_all[layer] = lax.dot_general(context, d_attn, CONTRACT_ROWS, preferred_element_type=jnp.float32)
        d_context = lax.dot_general(d_attn, wout_b[layer], CONTRACT_COLS, preferred_element_type=jnp.float32).astype(jnp.bfloat16).reshape(batch_loc, seq_len, heads_loc, head_dim)
        probs = attn_probs(query, key_blk, slope_loc, scale)
        d_probs = jnp.einsum('bqhd,bkhd->bhqk', d_context, value_blk, preferred_element_type=jnp.float32)
        d_value = jnp.einsum('bhqk,bqhd->bkhd', probs.astype(jnp.bfloat16), d_context, preferred_element_type=jnp.float32)
        d_scores = (probs * (d_probs - jnp.sum(probs * d_probs, axis=-1, keepdims=True)) * scale).astype(jnp.bfloat16)
        d_query = jnp.einsum('bhqk,bkhd->bqhd', d_scores, key_blk, preferred_element_type=jnp.float32)
        d_key = jnp.einsum('bhqk,bqhd->bkhd', d_scores, query, preferred_element_type=jnp.float32)
        d_qkv = jnp.stack([d_query, d_key, d_value], axis=3).reshape(n_tok, heads_loc * 3 * head_dim)
        g_bqkv_all[layer] = jnp.sum(d_qkv, axis=0).reshape(heads_loc, 3 * head_dim)
        d_qkv_b = d_qkv.astype(jnp.bfloat16)
        g_qkv_all[layer] = lax.dot_general(act_in, d_qkv_b, CONTRACT_ROWS, preferred_element_type=jnp.float32)
        d_norm_one = lax.psum(lax.dot_general(d_qkv_b, wqkv_b[layer], CONTRACT_COLS, preferred_element_type=jnp.float32), 'tp')
        d_res_ln, vec_grads[row_base], vec_grads[row_base + 1] = ln_one_vjp(d_norm_one)
        d_resid = d_mid + d_res_ln
    d_embed, vec_grads[0], vec_grads[1] = ln_zero_vjp(d_resid)
    d_rows = jnp.where(in_shard[:, None], d_embed, 0.0)
    g_emb = g_emb + jax.ops.segment_sum(d_rows, safe_ids, num_segments=vocab_loc)
    grads = [g_emb,
             jnp.stack([vec_grads[row] for row in range(final_row + 2)]),
             jnp.stack([g_qkv_all[layer] for layer in range(layers)]),
             jnp.stack([g_bqkv_all[layer] for layer in range(layers)]),
             jnp.stack([g_out_all[layer] for layer in range(layers)]),
             jnp.stack([g_up_all[layer] for layer in range(layers)]),
             jnp.stack([g_bup_all[layer] for layer in range(layers)]),
             jnp.stack([g_down_all[layer] for layer in range(layers)])]
    return loss_sum, grads


def solution(mesh):
    tp_size = mesh.shape['tp']
    dp_size = mesh.shape['dp']

    def device_step(tokens, labels, *state):
        masters = state[0:8]
        moms = state[8:16]
        vels = state[16:24]
        loss_sum, grads = local_grads(tokens, labels, masters, tp_size, dp_size)
        n_total = tokens.shape[0] * tokens.shape[1] * dp_size
        loss = lax.psum(loss_sum, 'dp') / n_total
        grads = [lax.psum(grad_arr, 'dp') for grad_arr in grads]
        sq_sharded = sum(jnp.sum(grads[slot] * grads[slot]) for slot in range(8) if slot != 1)
        sq_total = lax.psum(sq_sharded, 'tp') + jnp.sum(grads[1] * grads[1])
        clip_coef = jnp.minimum(1.0, CLIP_NORM / (jnp.sqrt(sq_total) + 1e-6))
        updated = [adam_update(masters[slot], grads[slot] * clip_coef, moms[slot], vels[slot], DECAYED[slot]) for slot in range(8)]
        new_masters = [entry[0] for entry in updated]
        new_moms = [entry[1] for entry in updated]
        new_vels = [entry[2] for entry in updated]
        new_bf16 = [entry.astype(jnp.bfloat16) for entry in new_masters]
        return (loss, *new_masters, *new_moms, *new_vels, *new_bf16)

    data_spec = P('dp', None)
    return jax.shard_map(device_step, mesh=mesh, in_specs=(data_spec, data_spec) + PARAM_SPECS * 3, out_specs=(P(),) + PARAM_SPECS * 4, check_vma=False)
```

profile of v0, /device:TPU:0, one launch (start us, length us, event | category | flops | bytes accessed | tf_op | source)
XLA Modules:
  0.0 2925.2 jit_solution(5383607800994305792)
XLA Ops:
  8.7 26.1 convert_element_type.161
  34.9 20.9 gather_fusion
  64.8 8.5 broadcast_multiply_fusion
  73.3 93.2 %all-reduce.15.cloned.1.call-done = f32[2048,512]{1,0:T(8,128)} async-done(((f32[2048,512]{1,0:T(8,128)}), f32[2048,512]{1,0:T(8,128)}) %all-reduce.15.cloned.1.call-update) | async-done | bytes 4194320 | tf_op jit(solution)/shard_map/psum | solution.py:85
  175.3 4.3 add_convert_fusion.1
  179.6 4.6 copy.104
  184.3 6.1 reshape.414
  190.4 4.3 fusion.182
  194.7 22.9 fusion.186
  217.7 12.3 fusion.106
  239.9 99.3 %all-reduce.17.cloned.1.call-done = f32[2048,512]{1,0:T(8,128)} async-done(((f32[2048,512]{1,0:T(8,128)}), f32[2048,512]{1,0:T(8,128)}) %all-reduce.17.cloned.1.call-update) | async-done | bytes 4194320 | tf_op jit(solution)/shard_map/psum | solution.py:100
  339.2 4.4 fusion.180
  351.4 4.6 fusion.119
  356.1 103.9 %all-reduce.19.cloned.1.call-done = f32[2048,512]{1,0:T(8,128)} async-done(((f32[2048,512]{1,0:T(8,128)}), f32[2048,512]{1,0:T(8,128)}) %all-reduce.19.cloned.1.call-update) | async-done | bytes 4194320 | tf_op jit(solution)/shard_map/psum | solution.py:107
  470.6 4.6 copy.110
  475.2 6.1 reshape.416
  481.3 4.3 fusion.181
  485.7 22.9 fusion.187
  508.6 12.3 fusion.103
  526.3 103.8 %all-reduce.21.cloned.1.call-done = f32[2048,512]{1,0:T(8,128)} async-done(((f32[2048,512]{1,0:T(8,128)}), f32[2048,512]{1,0:T(8,128)}) %all-reduce.21.cloned.1.call-update) | async-done | bytes 4194320 | tf_op jit(solution)/shard_map/psum | solution.py:100
  643.1 4.6 fusion.121
  648.4 103.3 %all-reduce.23.cloned.1.call-done = f32[2048,512]{1,0:T(8,128)} async-done(((f32[2048,512]{1,0:T(8,128)}), f32[2048,512]{1,0:T(8,128)}) %all-reduce.23.cloned.1.call-update) | async-done | bytes 4194320 | tf_op jit(solution)/shard_map/psum | solution.py:107
  758.6 79.6 %fusion.188 = (f32[2048]{0:T(1024)S(1)}, f32[2048,25152]{0,1:T(8,128)}) fusion(bf16[25152,512]{1,0:T(8,128)(2,1)} %convert_element_type.161, bf16[2048,512]{1,0:T(8,128)(2,1)S(1)} %add_convert_fusion.15.clone.4), kind=kOutput, calls=%fused_computation.310 | convolution fusion | flops 52799078400 | bytes 233906176 | tf_op jit(solution)/shard_map/dot_general | solution.py:113
  838.2 5.3 pmax.7
  843.6 62.5 %fusion.4 = (f32[2048]{0:T(1024)S(1)}, f32[2048]{0:T(1024)S(1)}) fusion(f32[2048,25152]{0,1:T(8,128)} %get-tuple-element.157, f32[2048]{0:T(1024)S(1)} %pmax.7, s32[2048]{0:T(1024)S(1)} %bitcast.246), kind=kLoop, calls=%fused_computation.10 | loop fusion | flops 257552384 | bytes 206077952 | tf_op jit(solution)/shard_map/reduce_sum | solution.py:116
  906.1 7.5 all-reduce.2
  913.7 98.2 %multiply_convert_fusion = bf16[2048,25152]{0,1:T(8,128)(2,1)} fusion(f32[2048,25152]{0,1:T(8,128)} %get-tuple-element.157, f32[2048]{0:T(1024)S(1)} %get-tuple-element.63, s32[2048]{0:T(1024)S(1)} %bitcast.247, f32[2048]{0:T(1024)S(1)} %pmax.7), kind=kLoop, calls=%fused_computation.6 | loop fusion | flops 360579072 | bytes 309092352 | tf_op jit(solution)/shard_map/convert_element_type | solution.py:122
  1011.9 63.1 %fusion.191 = f32[2048,512]{1,0:T(8,128)} fusion(bf16[2048,25152]{0,1:T(8,128)(2,1)} %multiply_convert_fusion, bf16[25152,512]{1,0:T(8,128)(2,1)} %convert_element_type.161), kind=kOutput, calls=%fused_computation.313 | convolution fusion | flops 52747567104 | bytes 132972544 | tf_op jit(solution)/shard_map/dot_general | solution.py:124
  1075.1 105.1 %all-reduce.25.cloned.1.call-done = f32[2048,512]{1,0:T(8,128)} async-done(((f32[2048,512]{1,0:T(8,128)}), f32[2048,512]{1,0:T(8,128)}) %all-reduce.25.cloned.1.call-update) | async-done | bytes 4194320 | tf_op jit(solution)/shard_map/psum | solution.py:124
  1180.2 5.3 multiply_reduce_fusion.3
  1191.7 8.6 fusion.189
  1202.3 4.5 fusion.71
  1207.0 103.8 %all-reduce.27.cloned.1.call-done = f32[2048,512]{1,0:T(8,128)} async-done(((f32[2048,512]{1,0:T(8,128)}), f32[2048,512]{1,0:T(8,128)}) %all-reduce.27.cloned.1.call-update) | async-done | bytes 4194320 | tf_op jit(solution)/shard_map/psum | solution.py:144
  1310.8 5.4 multiply_reduce_fusion.4
  1325.3 13.2 fusion.82
  1338.6 16.1 fusion.117
  1354.6 43.6 %fusion.94 = f32[2,1024,4,1,64]{1,4,2,0,3:T(8,128)} fusion(f32[2,4,1024,1024]{2,3,1,0:T(8,128)} %fusion.117, bf16[2,1024,4,1,64]{1,0,4,3,2:T(2,128)(2,1)} %get-tuple-element.125, f32[2,4,1024,1024]{2,3,1,0:T(8,128)} %get-tuple-element.155, f32[2,4,1024]{2,1,0:T(4,128)S(1)} %copy-done.141), kind=kOutput, calls=%fused_computation.158 | convolution fusion | flops 1132471296 | bytes 70287360 | tf_op jit(solution)/shard_map/bhqk,bqhd->bkhd/dot_general | solution.py:156
  1398.3 43.3 %fusion.91 = f32[2,1024,4,1,64]{1,4,2,0,3:T(8,128)} fusion(f32[2,4,1024,1024]{2,3,1,0:T(8,128)} %fusion.117, bf16[2,1024,4,1,64]{1,0,4,3,2:T(2,128)(2,1)S(1)} %copy-done.51, f32[2,4,1024,1024]{2,3,1,0:T(8,128)} %get-tuple-element.155, f32[2,4,1024]{2,1,0:T(4,128)S(1)} %copy-done.141), kind=kOutput, calls=%fused_computation.157 | convolution fusion | flops 1132471296 | bytes 70287360 | tf_op jit(solution)/shard_map/bhqk,bkhd->bqhd/dot_general | solution.py:155
  1455.6 102.8 %all-reduce.29.cloned.1.call-done = f32[2048,512]{1,0:T(8,128)} async-done(((f32[2048,512]{1,0:T(8,128)}), f32[2048,512]{1,0:T(8,128)}) %all-reduce.29.cloned.1.call-update) | async-done | bytes 4194320 | tf_op jit(solution)/shard_map/psum | solution.py:161
  1558.5 5.4 multiply_reduce_fusion.5
  1568.8 8.6 fusion.190
  1579.4 4.4 fusion.67
  1584.5 66.6 %fusion.149 = f32[25152,512]{1,0:T(8,128)} fusion(bf16[2048,25152]{0,1:T(8,128)(2,1)} %multiply_convert_fusion, f32[2048,512]{1,0:T(8,128)} %copy-done.11, f32[512]{0:T(512)S(1)} %bitcast.279, f32[512]{0:T(512)S(1)} %bitcast.261, f32[2048]{0:T(1024)S(1)} %copy-done.106, f32[2048]{0:T(1024)S(1)} %copy-done.88), kind=kOutput, calls=%fused_computation.279 | convolution fusion | flops 52752809984 | bytes 158748672 | tf_op jit(solution)/shard_map/dot_general | solution.py:123
  1651.2 7.4 fusion.73
  1658.7 8.6 convolution_bitcast_fusion
  1671.4 16.5 all-reduce.31.cloned.1.call-done
  1687.9 5.2 multiply_reduce_fusion.6
  1702.1 13.6 fusion.79
  1715.7 16.1 fusion.116
  1731.8 43.6 %fusion.88 = f32[2,1024,4,1,64]{1,4,2,0,3:T(8,128)} fusion(f32[2,4,1024,1024]{2,3,1,0:T(8,128)} %fusion.116, bf16[2,1024,4,1,64]{1,0,4,3,2:T(2,128)(2,1)} %get-tuple-element.128, f32[2,4,1024,1024]{2,3,1,0:T(8,128)} %get-tuple-element.153, f32[2,4,1024]{2,1,0:T(4,128)S(1)} %copy-done.139), kind=kOutput, calls=%fused_computation.156 | convolution fusion | flops 1132471296 | bytes 70287360 | tf_op jit(solution)/shard_map/bhqk,bqhd->bkhd/dot_general | solution.py:156
  1775.5 43.1 %fusion.85 = f32[2,1024,4,1,64]{1,4,2,0,3:T(8,128)} fusion(f32[2,4,1024,1024]{2,3,1,0:T(8,128)} %fusion.116, bf16[2,1024,4,1,64]{1,0,4,3,2:T(2,128)(2,1)S(1)} %copy-done.49, f32[2,4,1024,1024]{2,3,1,0:T(8,128)} %get-tuple-element.153, f32[2,4,1024]{2,1,0:T(4,128)S(1)} %copy-done.139), kind=kOutput, calls=%fused_computation.155 | convolution fusion | flops 1132471296 | bytes 70287360 | tf_op jit(solution)/shard_map/bhqk,bkhd->bqhd/dot_general | solution.py:155
  1836.0 5.2 fusion.76
  1844.9 4.3 convolution_bitcast_fusion.1
  1861.9 73.4 %all-reduce.33.cloned.1.call-done = f32[2048,512]{1,0:T(8,128)} async-done(((f32[2048,512]{1,0:T(8,128)}), f32[2048,512]{1,0:T(8,128)}) %all-reduce.33.cloned.1.call-update) | async-done | bytes 4194320 | tf_op jit(solution)/shard_map/psum | solution.py:161
  1935.4 5.3 multiply_reduce_fusion.7
  1950.3 46.4 %scatter_fusion = f32[25152,512]{1,0:T(8,128)} fusion(f32[25152,512]{1,0:T(8,128)} %fusion.149, s32[2048]{0:T(1024)S(1)} %bitcast.255, f32[2048,512]{1,0:T(8,128)} %add_select_fusion.4), kind=kCustom, calls=%fused_computation.1 | custom fusion | flops 1048576 | bytes 12591104 | tf_op jit(solution)/shard_map/scatter-add | solution.py:166
  2004.7 25.6 all-reduce
  2032.1 685.4 %all-reduce.35.cloned.1.call-done = (f32[25152,512]{1,0:T(8,128)}, f32[2,512,768]{2,1,0:T(8,128)}, f32[2,256,512]{2,1,0:T(8,128)}, f32[2,512,1024]{2,1,0:T(8,128)}, f32[2,1024,512]{2,1,0:T(8,128)}) async-done(((f32[25152,512]{1,0:T(8,128)}, f32[2,512,768]{2,1,0:T(8,128)}, f32[2,256,512]{2,1,0:T(8,128)}, f32[2,512,1024]{2,1,0:T(8,128)}, f32[2,1024,512]{2,1,0:T(8,128)}), (f32[25152,512]{1,0:T(8,128)}, ...) | async-done | bytes 64094224 | tf_op jit(solution)/shard_map/psum | solution.py:189
  2717.5 23.2 multiply_reduce_fusion
  2751.5 5.4 psum.174
  2758.4 125.1 %fusion.166 = (bf16[25152,512]{1,0:T(8,128)(2,1)}, f32[25152,512]{1,0:T(8,128)}, f32[25152,512]{1,0:T(8,128)}, f32[25152,512]{1,0:T(8,128)}) fusion(f32[25152,512]{1,0:T(8,128)} %param.29, f32[25152,512]{1,0:T(8,128)} %get-tuple-element.57, f32[]{:T(128)S(6)} %min.22, f32[25152,512]{1,0:T(8,128)} %param.37, f32[25152,512]{1,0:T(8,128)} %param.45), kind=kLoop, calls=%fused_computation.289 | loop fusion | flops 218923008 | bytes 386334720 | tf_op jit(solution)/shard_map/convert_element_type | solution.py:197
  2884.2 8.4 fusion.162
  2898.1 9.8 fusion.156
  2909.1 8.0 fusion.152
  (576 shorter events, 190.7 us)
Async XLA Ops:
  7.2 159.2 %all-reduce.15.cloned.1.call-start = ((), (), s32[]{:S(2)}) async-start(), calls=%async_computation | async-start | bytes 8388608 | tf_op jit(solution)/shard_map/psum | solution.py:85
  8.0 26.9 copy-start.125
  34.9 20.9 copy-start.156
  59.6 279.6 %all-reduce.17.cloned.1.call-start = ((), (), s32[]{:S(2)}) async-start(), calls=%async_computation.1 | async-start | bytes 8388608 | tf_op jit(solution)/shard_map/psum | solution.py:100
  64.7 110.6 %copy-start.154 = (f32[1,512]{1,0:T(1,128)}, f32[1,512]{1,0:T(1,128)S(1)}, u32[]{:S(2)}) copy-start(f32[1,512]{1,0:T(1,128)S(1)} %get-tuple-element.142) | copy-start | bytes 6148
  64.8 110.6 %copy-start.197 = (f32[1,512]{1,0:T(1,128)}, f32[1,512]{1,0:T(1,128)S(1)}, u32[]{:S(2)}) copy-start(f32[1,512]{1,0:T(1,128)S(1)} %get-tuple-element.141) | copy-start | bytes 6148
  64.8 274.4 %copy-start.107 = (f32[1,512]{1,0:T(1,128)}, f32[1,512]{1,0:T(1,128)S(1)}, u32[]{:S(2)}) copy-start(f32[1,512]{1,0:T(1,128)S(1)} %get-tuple-element.144) | copy-start | bytes 6148
  64.8 274.4 %copy-start.109 = (f32[1,512]{1,0:T(1,128)}, f32[1,512]{1,0:T(1,128)S(1)}, u32[]{:S(2)}) copy-start(f32[1,512]{1,0:T(1,128)S(1)} %get-tuple-element.143) | copy-start | bytes 6148
  64.8 280.8 %copy-start.158 = (f32[1,512]{1,0:T(1,128)}, f32[1,512]{1,0:T(1,128)S(1)}, u32[]{:S(2)}) copy-start(f32[1,512]{1,0:T(1,128)S(1)} %get-tuple-element.139) | copy-start | bytes 6148
  64.8 280.8 %copy-start.199 = (f32[1,512]{1,0:T(1,128)}, f32[1,512]{1,0:T(1,128)S(1)}, u32[]{:S(2)}) copy-start(f32[1,512]{1,0:T(1,128)S(1)} %get-tuple-element.138) | copy-start | bytes 6148
  64.8 400.8 %copy-start.161 = (f32[1,512]{1,0:T(1,128)}, f32[1,512]{1,0:T(1,128)S(1)}, u32[]{:S(2)}) copy-start(f32[1,512]{1,0:T(1,128)S(1)} %get-tuple-element.136) | copy-start | bytes 6148
  64.8 400.8 %copy-start.201 = (f32[1,512]{1,0:T(1,128)}, f32[1,512]{1,0:T(1,128)S(1)}, u32[]{:S(2)}) copy-start(f32[1,512]{1,0:T(1,128)S(1)} %get-tuple-element.135) | copy-start | bytes 6148
  169.0 170.2 %copy-start.82 = (f32[2048]{0:T(1024)}, f32[2048]{0:T(1024)S(1)}, u32[]{:S(2)}) copy-start(f32[2048]{0:T(1024)S(1)} %broadcast_multiply_fusion.6) | copy-start | bytes 24580
  172.1 167.1 %copy-start.84 = (f32[2048]{0:T(1024)}, f32[2048]{0:T(1024)S(1)}, u32[]{:S(2)}) copy-start(f32[2048]{0:T(1024)S(1)} %fusion.131) | copy-start | bytes 24580
  194.7 22.9 copy-start.48
  194.7 22.9 copy-start.46
  235.2 224.9 %all-reduce.19.cloned.1.call-start = ((), (), s32[]{:S(2)}) async-start(), calls=%async_computation.2 | async-start | bytes 8388608 | tf_op jit(solution)/shard_map/psum | solution.py:107
  239.9 105.7 %copy-start.65 = (bf16[2,512,1024]{2,1,0:T(8,128)(2,1)}, bf16[2,512,1024]{2,1,0:T(8,128)(2,1)S(1)}, u32[]{:S(2)}) copy-start(bf16[2,512,1024]{2,1,0:T(8,128)(2,1)S(1)} %convert_element_type.172) | copy-start | bytes 6291460
  239.9 108.3 %copy-start.189 = (f32[1,1024]{1,0:T(1,128)}, f32[1,1024]{1,0:T(1,128)S(1)}, u32[]{:S(2)}) copy-start(f32[1,1024]{1,0:T(1,128)S(1)} %get-tuple-element.147) | copy-start | bytes 12292
  239.9 400.0 %copy-start.193 = (f32[1,1024]{1,0:T(1,128)}, f32[1,1024]{1,0:T(1,128)S(1)}, u32[]{:S(2)}) copy-start(f32[1,1024]{1,0:T(1,128)S(1)} %get-tuple-element.146) | copy-start | bytes 12292
  356.0 274.1 %all-reduce.21.cloned.1.call-start = ((), (), s32[]{:S(2)}) async-start(), calls=%async_computation.3 | async-start | bytes 8388608 | tf_op jit(solution)/shard_map/psum | solution.py:100
  485.7 22.9 copy-start.50
  485.7 22.9 copy-start.47
  526.0 104.1 %copy-start.182 = (f32[1,512]{1,0:T(1,128)S(1)}, f32[1,512]{1,0:T(1,128)}, u32[]{:S(2)}) copy-start(f32[1,512]{1,0:T(1,128)} %get-tuple-element.134) | copy-start | bytes 6148
  526.1 225.7 %all-reduce.23.cloned.1.call-start = ((), (), s32[]{:S(2)}) async-start(), calls=%async_computation.4 | async-start | bytes 8388608 | tf_op jit(solution)/shard_map/psum | solution.py:107
  647.7 104.0 %copy-start.181 = (f32[1,512]{1,0:T(1,128)S(1)}, f32[1,512]{1,0:T(1,128)}, u32[]{:S(2)}) copy-start(f32[1,512]{1,0:T(1,128)} %get-tuple-element.131) | copy-start | bytes 6148
  647.7 532.5 %all-reduce.25.cloned.1.call-start = ((), (), s32[]{:S(2)}) async-start(), calls=%async_computation.5 | async-start | bytes 8388608 | tf_op jit(solution)/shard_map/psum | solution.py:124
  843.6 70.1 %copy-start.89 = (f32[2048]{0:T(1024)}, f32[2048]{0:T(1024)S(1)}, u32[]{:S(2)}) copy-start(f32[2048]{0:T(1024)S(1)} %pmax.7) | copy-start | bytes 24580
  913.7 98.2 %copy-start.136 = (f32[2048]{0:T(1024)}, f32[2048]{0:T(1024)S(1)}, u32[]{:S(2)}) copy-start(f32[2048]{0:T(1024)S(1)} %get-tuple-element.63) | copy-start | bytes 24580
  1075.0 105.2 %copy-start.87 = (f32[2048]{0:T(1024)S(1)}, f32[2048]{0:T(1024)}, u32[]{:S(2)}) copy-start(f32[2048]{0:T(1024)} %copy-done.86) | copy-start | bytes 24580
  1075.0 105.2 %copy-start.105 = (f32[2048]{0:T(1024)S(1)}, f32[2048]{0:T(1024)}, u32[]{:S(2)}) copy-start(f32[2048]{0:T(1024)} %copy-done.104) | copy-start | bytes 24580
  1075.0 105.2 %copy-start.152 = (f32[1,512]{1,0:T(1,128)S(1)}, f32[1,512]{1,0:T(1,128)}, u32[]{:S(2)}) copy-start(f32[1,512]{1,0:T(1,128)} %get-tuple-element.130) | copy-start | bytes 6148
  1075.0 110.5 %copy-start.124 = (f32[2048]{0:T(1024)S(1)}, f32[2048]{0:T(1024)}, u32[]{:S(2)}) copy-start(f32[2048]{0:T(1024)} %copy-done.123) | copy-start | bytes 24580
  1075.0 235.8 %all-reduce.27.cloned.1.call-start = ((), (), s32[]{:S(2)}) async-start(), calls=%async_computation.6 | async-start | bytes 8388608 | tf_op jit(solution)/shard_map/psum | solution.py:144
  1187.9 130.6 %copy-start.149 = (f32[2048]{0:T(1024)}, f32[2048]{0:T(1024)S(1)}, u32[]{:S(2)}) copy-start(f32[2048]{0:T(1024)S(1)} %negate_multiply_fusion.5) | copy-start | bytes 24580
  1206.8 104.1 %copy-start.102 = (f32[2048]{0:T(1024)S(1)}, f32[2048]{0:T(1024)}, u32[]{:S(2)}) copy-start(f32[2048]{0:T(1024)} %copy-done.101) | copy-start | bytes 24580
  1206.8 104.1 %copy-start.134 = (f32[2048]{0:T(1024)S(1)}, f32[2048]{0:T(1024)}, u32[]{:S(2)}) copy-start(f32[2048]{0:T(1024)} %copy-done.133) | copy-start | bytes 24580
  1206.8 104.1 %copy-start.165 = (f32[1,512]{1,0:T(1,128)S(1)}, f32[1,512]{1,0:T(1,128)}, u32[]{:S(2)}) copy-start(f32[1,512]{1,0:T(1,128)} %get-tuple-element.133) | copy-start | bytes 6148
  1206.8 109.4 %copy-start.122 = (f32[2048]{0:T(1024)S(1)}, f32[2048]{0:T(1024)}, u32[]{:S(2)}) copy-start(f32[2048]{0:T(1024)} %copy-done.121) | copy-start | bytes 24580
  1206.8 351.6 %all-reduce.29.cloned.1.call-start = ((), (), s32[]{:S(2)}) async-start(), calls=%async_computation.7 | async-start | bytes 8388608 | tf_op jit(solution)/shard_map/psum | solution.py:161
  1338.6 103.1 %copy-start.43 = (f32[2,1024,4,1,64]{1,4,2,0,3:T(8,128)}, f32[2,1024,4,1,64]{1,4,2,0,3:T(8,128)S(1)}, u32[]{:S(2)}) copy-start(f32[2,1024,4,1,64]{1,4,2,0,3:T(8,128)S(1)} %fusion.82) | copy-start | bytes 6291460
  1354.6 43.7 %copy-start.51 = (bf16[2,1024,4,1,64]{1,0,4,3,2:T(2,128)(2,1)S(1)}, bf16[2,1024,4,1,64]{1,0,4,3,2:T(2,128)(2,1)}, u32[]{:S(2)}) copy-start(bf16[2,1024,4,1,64]{1,0,4,3,2:T(2,128)(2,1)} %copy-done.50) | copy-start | bytes 3145732
  1454.4 104.1 %copy-start.99 = (f32[2048]{0:T(1024)S(1)}, f32[2048]{0:T(1024)}, u32[]{:S(2)}) copy-start(f32[2048]{0:T(1024)} %copy-done.98) | copy-start | bytes 24580
  1454.4 104.1 %copy-start.131 = (f32[2048]{0:T(1024)S(1)}, f32[2048]{0:T(1024)}, u32[]{:S(2)}) copy-start(f32[2048]{0:T(1024)} %copy-done.130) | copy-start | bytes 24580
  1454.4 104.1 %copy-start.162 = (f32[1,512]{1,0:T(1,128)S(1)}, f32[1,512]{1,0:T(1,128)}, u32[]{:S(2)}) copy-start(f32[1,512]{1,0:T(1,128)} %copy-done.161) | copy-start | bytes 6148
  1454.4 233.5 %all-reduce.31.cloned.1.call-start = ((), (), s32[]{:S(2)}) async-start(), calls=%async_computation.8 | async-start | bytes 8388608 | tf_op jit(solution)/shard_map/psum | solution.py:144
  1455.6 108.2 %copy-start.120 = (f32[2048]{0:T(1024)S(1)}, f32[2048]{0:T(1024)}, u32[]{:S(2)}) copy-start(f32[2048]{0:T(1024)} %copy-done.119) | copy-start | bytes 24580
  1583.9 67.3 %copy-start.103 = (f32[2048]{0:T(1024)S(1)}, f32[2048]{0:T(1024)}, u32[]{:S(2)}) copy-start(f32[2048]{0:T(1024)} %copy-done.101) | copy-start | bytes 24580
  1583.9 67.3 %copy-start.135 = (f32[2048]{0:T(1024)S(1)}, f32[2048]{0:T(1024)}, u32[]{:S(2)}) copy-start(f32[2048]{0:T(1024)} %copy-done.133) | copy-start | bytes 24580
  1583.9 67.3 %copy-start.166 = (f32[1,512]{1,0:T(1,128)S(1)}, f32[1,512]{1,0:T(1,128)}, u32[]{:S(2)}) copy-start(f32[1,512]{1,0:T(1,128)} %get-tuple-element.133) | copy-start | bytes 6148
  1583.9 67.3 %copy-start.204 = (f32[1,512]{1,0:T(1,128)S(1)}, f32[1,512]{1,0:T(1,128)}, u32[]{:S(2)}) copy-start(f32[1,512]{1,0:T(1,128)} %get-tuple-element.132) | copy-start | bytes 6148
  1583.9 351.5 %all-reduce.33.cloned.1.call-start = ((), (), s32[]{:S(2)}) async-start(), calls=%async_computation.9 | async-start | bytes 8388608 | tf_op jit(solution)/shard_map/psum | solution.py:161
  1667.4 20.5 copy-start.96
  1671.4 21.7 copy-start.118
  1715.7 102.8 %copy-start.45 = (f32[2,1024,4,1,64]{1,4,2,0,3:T(8,128)}, f32[2,1024,4,1,64]{1,4,2,0,3:T(8,128)S(1)}, u32[]{:S(2)}) copy-start(f32[2,1024,4,1,64]{1,4,2,0,3:T(8,128)S(1)} %fusion.79) | copy-start | bytes 6291460
  1731.8 43.7 %copy-start.49 = (bf16[2,1024,4,1,64]{1,0,4,3,2:T(2,128)(2,1)S(1)}, bf16[2,1024,4,1,64]{1,0,4,3,2:T(2,128)(2,1)}, u32[]{:S(2)}) copy-start(bf16[2,1024,4,1,64]{1,0,4,3,2:T(2,128)(2,1)} %copy-done.48) | copy-start | bytes 3145732
  1831.3 886.2 %all-reduce.35.cloned.1.call-start = ((), (), s32[]{:S(2)}) async-start(), calls=%async_computation.10 | async-start | bytes 128188416 | tf_op jit(solution)/shard_map/psum | solution.py:189
  1861.9 78.8 %copy-start.116 = (f32[2048]{0:T(1024)S(1)}, f32[2048]{0:T(1024)}, u32[]{:S(2)}) copy-start(f32[2048]{0:T(1024)} %copy-done.115) | copy-start | bytes 24580
  2717.5 23.2 copy-start.42
  2717.5 24.6 copy-start.59
  2758.3 125.1 %copy-start.94 = (f32[16,512]{1,0:T(8,128)S(1)}, f32[16,512]{1,0:T(8,128)}, u32[]{:S(2)}) copy-start(f32[16,512]{1,0:T(8,128)} %param.30) | copy-start | bytes 98308
  2758.3 125.1 %copy-start.143 = (f32[16,512]{1,0:T(8,128)S(1)}, f32[16,512]{1,0:T(8,128)}, u32[]{:S(2)}) copy-start(f32[16,512]{1,0:T(8,128)} %param.38) | copy-start | bytes 98308
  2758.3 125.1 %copy-start.144 = (f32[16,512]{1,0:T(8,128)S(1)}, f32[16,512]{1,0:T(8,128)}, u32[]{:S(2)}) copy-start(f32[16,512]{1,0:T(8,128)} %param.46) | copy-start | bytes 98308
  2758.4 125.8 %copy-start.41 = (f32[2,512,768]{2,1,0:T(8,128)S(1)}, f32[2,512,768]{2,1,0:T(8,128)}, u32[]{:S(2)}) copy-start(f32[2,512,768]{2,1,0:T(8,128)} %param.31) | copy-start | bytes 9437188
  (162 other events, 754.6 us)
Sparse Core Ops, SparseCore 0:
  59.7 106.7 all-reduce.14
  235.3 103.8 all-reduce.16
  356.1 103.8 all-reduce.18
  526.2 103.8 all-reduce.20
  647.8 103.8 all-reduce.22
  1075.2 104.9 all-reduce.24
  1206.9 103.8 all-reduce.26
  1454.5 103.8 all-reduce.28
  1584.0 103.8 all-reduce.30
  1831.4 103.8 all-reduce.32
  1996.9 720.5 all-reduce.34
where the time goes:
time: 2930 us
  waiting for transfers between devices  1590 us (54%)
  matrix products  612 us (21%)
  other arithmetic  537 us (18%)
  local copies, waits for them, and re-layouts  116 us (4%)
  blocking collectives  43.9 us (1%)
    psum x1, waiting for transfers between devices, device_step(): grads = [lax.psum(grad_arr, 'dp') for grad_arr in grads]  685 us
    psum x2, waiting for transfers between devices, local_grads(): lax.psum(jnp.dot(hidden, wdown_b[layer], preferred_element_type=jnp.float...  207 us
    psum x2, waiting for transfers between devices, local_grads(): lax.psum(jnp.dot(context, wout_b[layer], preferred_element_type=jnp.float...  203 us
    psum x2, waiting for transfers between devices, local_grads(): lax.psum(lax.dot_general(d_qkv_b, wqkv_b[layer], CONTRACT_COLS, preferred...  176 us
    convert_element_type x8, other arithmetic, device_step(): new_bf16 = [entry.astype(jnp.bfloat16) for entry in new_masters]  156 us
    psum x2, waiting for transfers between devices, local_grads(): lax.psum(lax.dot_general(d_pre_b, wup_b[layer], CONTRACT_COLS, preferred_...  120 us
    psum x1, waiting for transfers between devices, local_grads(): lax.psum(jnp.dot(d_logits, emb_b, preferred_element_type=jnp.float32), 'tp')  105 us
    convert_element_type x1, other arithmetic, local_grads(): ((shifted / sum_exp[:, None] - onehot.astype(jnp.float32)) / n_total).ast...  98.2 us
  transfers between devices with their start and end apart: 11, of which 11 were waited for; matrix products, arithmetic and copies ran while one was open for 5% of the time, Pallas kernels for 0%

commit v1 on v0

v1 whole, which is shorter than its diff:
```python
import functools
import math
import jax
import jax.numpy as jnp
from jax import lax
from jax.experimental import pallas as pl
from jax.experimental.pallas import tpu as pltpu
from jax.sharding import PartitionSpec as P

ZERO, ONE, TWO, THREE, FOUR = range(5)
LANES = 128
LN_EPS = 1e-5
CLIP_NORM = 1.0
BETA_ONE = 0.9
BETA_TWO = 0.95
ADAM_EPS = 1e-8
WEIGHT_DECAY = 0.1
LEARN_RATE = 1e-3
STEP_COUNT = 10
DECAYED = (True, False, True, False, True, True, False, True)
PARAM_SPECS = (P('tp', None), P(None, None), P(None, None, 'tp'), P(None, 'tp', None), P(None, 'tp', None), P(None, None, 'tp'), P(None, 'tp'), P(None, 'tp', None))
NT = (((ONE,), (ONE,)), ((), ()))
NN = (((ONE,), (ZERO,)), ((), ()))
TN = (((ZERO,), (ZERO,)), ((), ()))
f32 = jnp.float32
bf16 = jnp.bfloat16
MESH = pl.DeviceIdType.MESH
MIB = TWO ** 20
COST = pl.CostEstimate(flops=10 ** 6, bytes_accessed=10 ** 6, transcendentals=ZERO)


def alibi_slopes(heads):
    closest = TWO ** int(math.floor(math.log2(heads)))
    first_base = 2.0 ** (-8.0 / closest)
    slopes = [first_base ** (head_idx + ONE) for head_idx in range(closest)]
    extra_base = 2.0 ** (-4.0 / closest)
    extra_count = min(closest, heads - closest)
    return slopes + [extra_base ** (TWO * head_idx + ONE) for head_idx in range(extra_count)]


def layer_norm(values, gain, bias):
    centred = values - jnp.mean(values, axis=-ONE, keepdims=True)
    variance = jnp.mean(centred * centred, axis=-ONE, keepdims=True)
    return centred * lax.rsqrt(variance + LN_EPS) * gain + bias


def gelu_tanh(values):
    return jax.nn.gelu(values, approximate=True)


def dot(a, b, dims):
    return lax.dot_general(a, b, dims, preferred_element_type=f32)


def adam_update(master, grad_arr, moment, velocity, decayed):
    mom_new = BETA_ONE * moment + (1.0 - BETA_ONE) * grad_arr
    vel_new = BETA_TWO * velocity + (1.0 - BETA_TWO) * grad_arr * grad_arr
    mom_hat = mom_new / (1.0 - BETA_ONE ** STEP_COUNT)
    vel_hat = vel_new / (1.0 - BETA_TWO ** STEP_COUNT)
    direction = mom_hat / (jnp.sqrt(vel_hat) + ADAM_EPS)
    if decayed:
        direction = direction + WEIGHT_DECAY * master
    return master - LEARN_RATE * direction, mom_new, vel_new


WIDE = 256


def share_plan(shapes):
    plan, at = [], ZERO
    for i, (r, c) in enumerate(shapes):
        for j in range(c // WIDE):
            plan.append((i, at, r, j))
            at += r
    return plan, at


def pack_kernel(pos_ref, *refs):
    ins, out = refs[:-ONE], refs[-ONE]
    plan, _ = share_plan([r.shape[ONE:] for r in ins])
    for i, at, r, j in plan:
        out[at:at + r, :] = ins[i][ZERO, :, j * WIDE:(j + ONE) * WIDE]


def pack_share(pos, ws, layer, ndp):
    blocks = [(w.shape[ONE] // ndp, w.shape[TWO]) for w in ws]
    rows = share_plan(blocks)[ONE]
    return pl.pallas_call(
        pack_kernel,
        grid_spec=pltpu.PrefetchScalarGridSpec(
            num_scalar_prefetch=ONE, grid=(ONE,),
            in_specs=[pl.BlockSpec((ONE,) + b, lambda i, p: (layer, p[ZERO], ZERO)) for b in blocks],
            out_specs=pl.BlockSpec((rows, WIDE), lambda i, p: (ZERO, ZERO))),
        out_shape=jax.ShapeDtypeStruct((rows, WIDE), f32),
        cost_estimate=COST,
        name="pack_share")(pos, *ws)


def join_kernel(oth_ref, *refs, hd):
    own, (wd, wu, wo, wq) = refs[:FOUR], refs[FOUR:]
    plan, _ = share_plan([r.shape[ONE:] for r in own])
    oth = [jnp.concatenate([oth_ref[ZERO, at:at + r, :] for i, at, r, j in plan if i == k], axis=ONE) for k in range(FOUR)]
    wd[ZERO], wd[ONE] = own[ZERO][ZERO].astype(bf16), oth[ZERO].astype(bf16)
    wo[ZERO], wo[ONE] = own[TWO][ZERO].astype(bf16), oth[TWO].astype(bf16)
    c = own[ONE].shape[TWO]
    wu[:, :c], wu[:, c:] = own[ONE][ZERO].astype(bf16), oth[ONE].astype(bf16)
    mine, heads = own[THREE][ZERO], own[THREE].shape[TWO] // (THREE * hd)
    for kind in range(THREE):
        cols = [src[:, (THREE * h + kind) * hd:(THREE * h + kind + ONE) * hd] for src in (mine, oth[THREE]) for h in range(heads)]
        width = TWO * heads * hd
        wq[:, kind * width:(kind + ONE) * width] = jnp.concatenate(cols, axis=ONE).astype(bf16)


def join_halves(oth, ws, layer, hd):
    ndp, rows, _ = oth.shape
    blocks = [(w.shape[ONE] // ndp, w.shape[TWO]) for w in ws]
    d, u, o, q = [(w.shape[ONE], w.shape[TWO]) for w in ws]
    stacked = lambda b: pl.BlockSpec((TWO,) + b, lambda p: (ZERO, p, ZERO))
    wide = lambda b: pl.BlockSpec((b[ZERO], TWO * b[ONE]), lambda p: (p, ZERO))
    wd, wu, wo, wq = pl.pallas_call(
        functools.partial(join_kernel, hd=hd), grid=(ndp,),
        in_specs=[pl.BlockSpec((ONE, rows, WIDE), lambda p: (p, ZERO, ZERO))] + [pl.BlockSpec((ONE,) + b, lambda p: (layer, p, ZERO)) for b in blocks],
        out_specs=[stacked(blocks[ZERO]), wide(blocks[ONE]), stacked(blocks[TWO]), wide(blocks[THREE])],
        out_shape=[jax.ShapeDtypeStruct(x, bf16) for x in ((TWO,) + d, (u[ZERO], TWO * u[ONE]), (TWO,) + o, (q[ZERO], TWO * q[ONE]))],
        compiler_params=pltpu.CompilerParams(dimension_semantics=("arbitrary",), vmem_limit_bytes=32 * MIB),
        cost_estimate=COST,
        name="join_halves")(oth, *ws)
    return wd.reshape(TWO * d[ZERO], d[ONE]), wu, wo.reshape(TWO * o[ZERO], o[ONE]), wq


def wgrad_mlp_kernel(z_ref, hid, d_out, mlp_in, d_pre, out):
    ndp = out.shape[ONE]
    g = dot(hid[:], d_out[:], TN)
    r, at = g.shape[ZERO] // ndp, ZERO
    for j in range(g.shape[ONE] // WIDE):
        for p in range(ndp):
            out[ZERO, p, at:at + r, :] = g[p * r:(p + ONE) * r, j * WIDE:(j + ONE) * WIDE]
        at += r
    g = dot(mlp_in[:], d_pre[:], TN)
    r = g.shape[ZERO] // ndp
    for j in range(g.shape[ONE] // WIDE):
        for p in range(ndp):
            out[ZERO, p, at:at + r, :] = g[p * r:(p + ONE) * r, j * WIDE:(j + ONE) * WIDE]
        at += r


def wgrad_attn_kernel(z_ref, ctx, d_attn, act_in, d_q, d_k, d_v, prev, out):
    ndp = out.shape[ONE]
    g = dot(ctx[:], d_attn[:], TN)
    r, at = g.shape[ZERO] // ndp, ZERO
    for j in range(g.shape[ONE] // WIDE):
        for p in range(ndp):
            out[ZERO, p, at:at + r, :] = g[p * r:(p + ONE) * r, j * WIDE:(j + ONE) * WIDE]
        at += r
    for part in (d_q, d_k, d_v):
        g = dot(act_in[:], part[:], TN)
        r = g.shape[ZERO] // ndp
        for j in range(g.shape[ONE] // WIDE):
            for p in range(ndp):
                out[ZERO, p, at:at + r, :] = g[p * r:(p + ONE) * r, j * WIDE:(j + ONE) * WIDE]
            at += r


def wgrad(kernel, z, split, ops, ndp, rows, first, total, prev):
    tok = ops[ZERO].shape[ZERO]
    specs = [pl.BlockSpec((tok, op.shape[ONE] // TWO), lambda i, zr: (ZERO, i)) if cut else pl.BlockSpec(op.shape, lambda i, zr: (ZERO, ZERO)) for op, cut in zip(ops, split)]
    aliases, extra = {}, []
    if prev is not None:
        aliases, extra = {ONE + len(ops): ZERO}, [prev]
        specs.append(pl.BlockSpec(memory_space=pl.ANY))
    return pl.pallas_call(
        kernel,
        grid_spec=pltpu.PrefetchScalarGridSpec(
            num_scalar_prefetch=ONE, grid=(TWO,), in_specs=specs,
            out_specs=pl.BlockSpec((ONE, ndp, rows, WIDE), lambda i, zr: (lax.rem(i + zr[ZERO], TWO), ZERO, first // rows, ZERO))),
        out_shape=jax.ShapeDtypeStruct((TWO, ndp, total, WIDE), f32),
        input_output_aliases=aliases,
        compiler_params=pltpu.CompilerParams(dimension_semantics=("arbitrary",), vmem_limit_bytes=48 * MIB),
        cost_estimate=COST)(z, *ops, *extra)


def adam_layers_kernel(clip_ref, g_ref, *refs, hd):
    states, outs = refs[:12], refs[12:]
    shapes = [r.shape[ONE:] for r in states[:FOUR]]
    plan, _ = share_plan(shapes)
    for k in range(FOUR):
        parts = [g_ref[ZERO, at:at + r, :] for i, at, r, j in plan if i == k]
        if k == THREE:
            heads = shapes[THREE][ONE] // (THREE * hd)
            parts = [parts[kind][:, h * hd:(h + ONE) * hd] for h in range(heads) for kind in range(THREE)]
        g = jnp.concatenate(parts, axis=ONE) * clip_ref[ZERO]
        new, mom, vel = adam_update(states[k][ZERO], g, states[FOUR + k][ZERO], states[8 + k][ZERO], True)
        outs[k][ZERO], outs[FOUR + k][ZERO], outs[8 + k][ZERO], outs[12 + k][ZERO] = new, mom, vel, new.astype(bf16)


def adam_layers(clip, g, ws, ms, vs, layers, hd):
    ndp = g.shape[ZERO]
    rows = g.shape[ONE] // layers
    blocks = [pl.BlockSpec((ONE, w.shape[ONE] // ndp, w.shape[TWO]), lambda la, p: (la, p, ZERO)) for w in ws]
    shapes = [jax.ShapeDtypeStruct(w.shape, f32) for w in ws]
    return pl.pallas_call(
        functools.partial(adam_layers_kernel, hd=hd), grid=(layers, ndp),
        in_specs=[pl.BlockSpec(memory_space=pltpu.SMEM), pl.BlockSpec((ONE, rows, WIDE), lambda la, p: (p, la, ZERO))] + blocks * THREE,
        out_specs=blocks * FOUR,
        out_shape=shapes * THREE + [jax.ShapeDtypeStruct(w.shape, bf16) for w in ws],
        compiler_params=pltpu.CompilerParams(dimension_semantics=("arbitrary", "arbitrary"), vmem_limit_bytes=40 * MIB),
        cost_estimate=COST,
        name="adam_layers")(clip, g, *ws, *ms, *vs)


def gather_kernel(ids_ref, emb, out, buf, sem):
    n = out.shape[ZERO]

    def go(i, carry):
        pltpu.make_async_copy(emb.at[pl.ds(ids_ref[i], ONE)], buf.at[pl.ds(i, ONE)], sem).start()
        return carry

    lax.fori_loop(ZERO, n, go, ZERO, unroll=16)
    pltpu.make_async_copy(emb.at[pl.ds(ZERO, n)], buf, sem).wait()
    out[:] = buf[:].astype(bf16).astype(f32)


def gather_rows(ids, emb):
    n, dim = ids.shape[ZERO], emb.shape[ONE]
    return pl.pallas_call(
        gather_kernel, in_specs=[pl.BlockSpec(memory_space=pltpu.SMEM), pl.BlockSpec(memory_space=pl.ANY)],
        out_specs=pl.BlockSpec(memory_space=pltpu.VMEM), out_shape=jax.ShapeDtypeStruct((n, dim), f32),
        scratch_shapes=[pltpu.VMEM((n, dim), f32), pltpu.SemaphoreType.DMA],
        compiler_params=pltpu.CompilerParams(vmem_limit_bytes=20 * MIB),
        cost_estimate=COST,
        name="gather_rows")(ids, emb)


def slab_kernel(idx_ref, emb, out, buf, sems):
    _, live, dim = buf.shape
    half = out.shape[ZERO] // TWO
    copies = [pltpu.make_async_copy(emb.at[pl.ds(pl.multiple_of(idx_ref[i] * live, 8), live)], buf.at[i], sems.at[i]) for i in range(TWO)]
    for copy in copies:
        copy.start()
    for i, copy in enumerate(copies):
        copy.wait()
        out[i * half:i * half + live, :] = buf[i].astype(bf16)
        out[i * half + live:(i + ONE) * half, :] = jnp.zeros((half - live, dim), bf16)


def make_slab(idx, emb, live, half):
    dim = emb.shape[ONE]
    return pl.pallas_call(
        slab_kernel, in_specs=[pl.BlockSpec(memory_space=pltpu.SMEM), pl.BlockSpec(memory_space=pl.ANY)],
        out_specs=pl.BlockSpec(memory_space=pltpu.VMEM), out_shape=jax.ShapeDtypeStruct((TWO * half, dim), bf16),
        scratch_shapes=[pltpu.VMEM((TWO, live, dim), f32), pltpu.SemaphoreType.DMA((TWO,))],
        compiler_params=pltpu.CompilerParams(vmem_limit_bytes=32 * MIB),
        cost_estimate=COST,
        name="make_slab")(idx, emb)


def attn_probs(k, q, slope, row0, tri):
    kv, blk = k.shape[ZERO], q.shape[ZERO]
    jpos = lax.broadcasted_iota(jnp.int32, (kv, ONE), ZERO).astype(f32)
    s = dot(k, q, NT) + slope * (jpos - float(row0))
    diag = jnp.where(tri, s[kv - blk:, :], -jnp.inf)
    s = diag if kv == blk else jnp.concatenate([s[:kv - blk, :], diag], axis=ZERO)
    e = jnp.exp(s - jnp.max(s, axis=ZERO, keepdims=True))
    return e * (1.0 / jnp.sum(e, axis=ZERO, keepdims=True))


def attn_fwd_kernel(slope_ref, q_ref, k_ref, v_ref, o_ref, *, blk, hd):
    pair = pl.program_id(ZERO)
    lane = lax.broadcasted_iota(jnp.int32, (ONE, TWO * hd), ONE)
    tri = lax.broadcasted_iota(jnp.int32, (blk, blk), ZERO) <= lax.broadcasted_iota(jnp.int32, (blk, blk), ONE)
    for i in reversed(range(q_ref.shape[ZERO] // blk)):
        kv = (i + ONE) * blk
        q, k, v = q_ref[i * blk:kv, :], k_ref[:kv, :], v_ref[:kv, :]
        outs = []
        for a in range(TWO):
            sel = (lane >= hd) if a else (lane < hd)
            qa = jnp.where(sel, q, jnp.zeros_like(q)) * jnp.asarray(hd ** -0.5, bf16)
            p = attn_probs(k, qa, slope_ref[TWO * pair + a], i * blk, tri)
            outs.append(dot(p.astype(bf16), v, TN))
        o_ref[i * blk:kv, :] = jnp.where(lane < hd, outs[ZERO], outs[ONE]).astype(bf16)


def attn_bwd_kernel(slope_ref, q_ref, k_ref, v_ref, do_ref, dq_ref, dk_ref, dv_ref, db_ref, dkacc, dvacc, *, blk, hd):
    pair = pl.program_id(ZERO)
    n = q_ref.shape[ZERO] // blk
    scale = hd ** -0.5
    lane = lax.broadcasted_iota(jnp.int32, (ONE, TWO * hd), ONE)
    tri = lax.broadcasted_iota(jnp.int32, (blk, blk), ZERO) <= lax.broadcasted_iota(jnp.int32, (blk, blk), ONE)
    qsum = jnp.zeros((ONE, TWO * hd), f32)
    for i in reversed(range(n)):
        kv = (i + ONE) * blk
        q, do = q_ref[i * blk:kv, :], do_ref[i * blk:kv, :]
        k, v = k_ref[:kv, :], v_ref[:kv, :]
        dqs, dks, dvs = [], [], []
        for a in range(TWO):
            sel = (lane >= hd) if a else (lane < hd)
            qs = jnp.where(sel, q, jnp.zeros_like(q))
            doa = jnp.where(sel, do, jnp.zeros_like(do))
            p = attn_probs(k, qs * jnp.asarray(scale, bf16), slope_ref[TWO * pair + a], i * blk, tri)
            pdp = p * dot(v, doa, NT)
            delta = jnp.sum(pdp, axis=ZERO, keepdims=True)
            ds = ((pdp - p * delta) * scale).astype(bf16)
            dvs.append(dot(p.astype(bf16), doa, NN))
            dks.append(dot(ds, qs, NN))
            dqs.append(dot(ds, k, TN))
        dq = jnp.where(lane < hd, dqs[ZERO], dqs[ONE])
        qsum = qsum + jnp.sum(dq, axis=ZERO, keepdims=True)
        dq_ref[i * blk:kv, :] = dq.astype(bf16)
        if i == n - ONE:
            dkacc[:] = dks[ZERO] + dks[ONE]
            dvacc[:] = dvs[ZERO] + dvs[ONE]
        else:
            dkacc[:kv, :] += dks[ZERO] + dks[ONE]
            dvacc[:kv, :] += dvs[ZERO] + dvs[ONE]
    dk_ref[:] = dkacc[:].astype(bf16)
    dv_ref[:] = dvacc[:].astype(bf16)
    db_ref[ZERO:ONE, :] = qsum
    db_ref[ONE:TWO, :] = jnp.sum(dkacc[:], axis=ZERO, keepdims=True)
    db_ref[TWO:THREE, :] = jnp.sum(dvacc[:], axis=ZERO, keepdims=True)
    db_ref[THREE:8, :] = jnp.zeros((5, TWO * hd), f32)


def attn_fwd(qkv, slopes, hd, blk):
    seq, width = qkv.shape
    dim = width // THREE
    npair = dim // (TWO * hd)
    spec = lambda off: pl.BlockSpec((seq, TWO * hd), lambda h: (ZERO, h + off))
    return pl.pallas_call(
        functools.partial(attn_fwd_kernel, blk=blk, hd=hd), grid=(npair,),
        in_specs=[pl.BlockSpec(memory_space=pltpu.SMEM), spec(ZERO), spec(npair), spec(TWO * npair)],
        out_specs=spec(ZERO), out_shape=jax.ShapeDtypeStruct((seq, dim), bf16),
        compiler_params=pltpu.CompilerParams(dimension_semantics=("arbitrary",), vmem_limit_bytes=40 * MIB),
        cost_estimate=COST,
        name="attn_fwd")(slopes, qkv, qkv, qkv)


def attn_bwd(qkv, d_ctx, slopes, hd, blk):
    seq, width = qkv.shape
    dim = width // THREE
    npair = dim // (TWO * hd)
    spec = lambda off: pl.BlockSpec((seq, TWO * hd), lambda h: (ZERO, h + off))
    return pl.pallas_call(
        functools.partial(attn_bwd_kernel, blk=blk, hd=hd), grid=(npair,),
        in_specs=[pl.BlockSpec(memory_space=pltpu.SMEM), spec(ZERO), spec(npair), spec(TWO * npair), spec(ZERO)],
        out_specs=[spec(ZERO)] * THREE + [pl.BlockSpec((8, TWO * hd), lambda h: (ZERO, h))],
        out_shape=[jax.ShapeDtypeStruct((seq, dim), bf16)] * THREE + [jax.ShapeDtypeStruct((8, dim), f32)],
        scratch_shapes=[pltpu.VMEM((seq, TWO * hd), f32)] * TWO,
        compiler_params=pltpu.CompilerParams(dimension_semantics=("arbitrary",), vmem_limit_bytes=48 * MIB),
        cost_estimate=COST,
        name="attn_bwd")(slopes, qkv, qkv, qkv, d_ctx)


def head_fwd_kernel(*refs, npiece, nself, vb, half, live):
    e_ref, h_refs = refs[ZERO], refs[ONE:ONE + npiece]
    m_ref, s_ref, hb_ref, hs, la, lb, acc = refs[-7:]
    sums = refs[-8 - (ZERO < nself < npiece):-7]
    step = pl.program_id(ZERO)
    nvoc, nb = e_ref.shape[ZERO], e_ref.shape[ZERO] // vb
    for i in range(npiece):
        @pl.when(step == i)
        def _(i=i):
            hs[:] = h_refs[i][:].astype(bf16)
    h = hs[:]
    hb_ref[:] = h
    bufs = (la, lb)

    def logits(b):
        bufs[b % TWO][:] = dot(h, e_ref[b * vb:(b + ONE) * vb, :], NT)

    def drop_padding(b):
        buf = bufs[b % TWO]
        for hh in range(nvoc // half):
            lo, hi = max(hh * half + live - b * vb, ZERO), min((hh + ONE) * half - b * vb, vb)
            if lo < hi:
                a0, a1 = lo // LANES * LANES, -(-hi // LANES) * LANES
                col = lax.broadcasted_iota(jnp.int32, (ONE, a1 - a0), ONE) + a0
                buf[:, a0:a1] = jnp.where((col >= lo) & (col < hi), -jnp.inf, buf[:, a0:a1])

    top = total = None
    logits(ZERO)
    for b in range(nb):
        if b + ONE < nb:
            logits(b + ONE)
        drop_padding(b)
        lg = bufs[b % TWO][:]
        e = e_ref[b * vb:(b + ONE) * vb, :]
        blk_top = jnp.max(lg, axis=ONE, keepdims=True)
        if b == ZERO:
            top = blk_top
            p = jnp.exp(lg - top)
            total = jnp.sum(p, axis=ONE, keepdims=True)
            acc[:] = dot(p.astype(bf16), e, NN)
        else:
            new = jnp.maximum(top, blk_top)
            alpha = jnp.exp(top - new)
            p = jnp.exp(lg - new)
            total = total * alpha + jnp.sum(p, axis=ONE, keepdims=True)
            acc[:] = acc[:] * alpha + dot(p.astype(bf16), e, NN)
            top = new
    m_ref[:] = jnp.transpose(top)[None]
    s_ref[:] = jnp.transpose(total)[None]

    if len(sums) == ONE:
        sums[ZERO][:] = acc[:]
    else:
        @pl.when(step < nself)
        def _():
            sums[ZERO][:] = acc[:]

        @pl.when(step >= nself)
        def _():
            sums[ONE][:] = acc[:]


def head_fwd(slab, self_pieces, core_pieces, hb, pos, total_pieces, t, live, vb):
    pieces = list(self_pieces) + list(core_pieces)
    n, k = len(pieces), len(self_pieces)
    nvoc, dim = slab.shape
    ins = [slab] + [arr for arr, _ in pieces]
    in_specs = [pl.BlockSpec((nvoc, dim), lambda i: (ZERO, ZERO))] + [pl.BlockSpec((t, dim), lambda i, blk=blk: (blk, ZERO)) for _, blk in pieces]
    row = pl.BlockSpec((ONE, ONE, t), lambda i: (i, ZERO, ZERO))
    out_specs, out_shape = [], []
    if k:
        out_specs.append(pl.BlockSpec((t, dim), lambda i: (jnp.minimum(i, k - ONE), ZERO)))
        out_shape.append(jax.ShapeDtypeStruct((k * t, dim), f32))
    if n > k:
        out_specs.append(pl.BlockSpec((t, dim), lambda i: (jnp.maximum(i - k, ZERO), ZERO)))
        out_shape.append(jax.ShapeDtypeStruct(((n - k) * t, dim), f32))
    out_specs += [row, row, pl.BlockSpec((t, dim), lambda i: (i + pos, ZERO))]
    stats = jax.ShapeDtypeStruct((n, ONE, t), f32)
    out_shape += [stats, stats, jax.ShapeDtypeStruct((total_pieces * t, dim), bf16)]
    aliases = {}
    if hb is not None:
        aliases = {len(ins): len(out_shape) - ONE}
        ins.append(hb)
        in_specs.append(pl.BlockSpec(memory_space=pl.ANY))
    return pl.pallas_call(
        functools.partial(head_fwd_kernel, npiece=n, nself=k, vb=vb, half=nvoc // TWO, live=live), grid=(n,),
        in_specs=in_specs, out_specs=out_specs, out_shape=out_shape,
        scratch_shapes=[pltpu.VMEM((t, dim), bf16), pltpu.VMEM((t, vb), f32), pltpu.VMEM((t, vb), f32), pltpu.VMEM((t, dim), f32)],
        input_output_aliases=aliases,
        compiler_params=pltpu.CompilerParams(dimension_semantics=("arbitrary",), vmem_limit_bytes=58 * MIB),
        cost_estimate=COST,
        name="head_fwd")(*ins)


def head_grad_kernel(base_ref, e_ref, h_ref, lse_ref, lab_ref, g_ref, *, tt, sub, inv):
    vb = e_ref.shape[ZERO]
    base = base_ref[ZERO] + pl.program_id(ZERO) * vb

    def step(t, carry):
        h = h_ref[pl.ds(pl.multiple_of(t * tt, tt), tt), :]
        lse, lab = lse_ref[t], lab_ref[t]
        for r in range(vb // sub):
            row = lax.broadcasted_iota(jnp.int32, (sub, ONE), ZERO) + (base + r * sub)
            p = jnp.exp(dot(e_ref[r * sub:(r + ONE) * sub, :], h, NT) - lse)
            d = jnp.where(row == lab, p - 1.0, p).astype(bf16)
            g_ref[r * sub:(r + ONE) * sub, :] += dot(d, h, NN)
        return carry

    g_ref[:] = jnp.zeros_like(g_ref)
    lax.fori_loop(ZERO, h_ref.shape[ZERO] // tt, step, ZERO)
    g_ref[:] *= inv


def head_grad(base, slab, first_block, nblocks, h, lse, lab, vb, tt, sub, inv):
    ntok, dim = h.shape
    n = ntok // tt
    return pl.pallas_call(
        functools.partial(head_grad_kernel, tt=tt, sub=sub, inv=inv), grid=(nblocks,),
        in_specs=[pl.BlockSpec(memory_space=pltpu.SMEM), pl.BlockSpec((vb, dim), lambda b: (b + first_block, ZERO)),
                  pl.BlockSpec((ntok, dim), lambda b: (ZERO, ZERO)),
                  pl.BlockSpec((n, ONE, tt), lambda b: (ZERO, ZERO, ZERO)), pl.BlockSpec((n, ONE, tt), lambda b: (ZERO, ZERO, ZERO))],
        out_specs=pl.BlockSpec((vb, dim), lambda b: (b, ZERO)),
        out_shape=jax.ShapeDtypeStruct((nblocks * vb, dim), f32),
        compiler_params=pltpu.CompilerParams(dimension_semantics=("arbitrary",), vmem_limit_bytes=58 * MIB),
        cost_estimate=COST,
        name="head_grad")(base, slab, h, lse, lab)


def scatter_kernel(count_ref, key_ref, d_hbm, *refs, chunk, depth, ring, nin, rows):
    own_refs, g_refs, (*g_outs, sq_ref, acc, buf, sems) = refs[:nin], refs[nin:TWO * nin], refs[TWO * nin:]
    n = count_ref[ZERO]
    acc[:] = jnp.zeros_like(acc)
    nchunk = (n + chunk - ONE) // chunk

    def fetch(c):
        slot = c % ring

        def one(i, carry):
            pltpu.make_async_copy(d_hbm.at[key_ref[c * chunk + i] // depth], buf.at[slot, i], sems.at[slot]).start()
            return carry

        lax.fori_loop(ZERO, chunk, one, ZERO, unroll=16)

    for c in range(ring - ONE):
        @pl.when(c < nchunk)
        def _(c=c):
            fetch(c)

    def body(c, carry):
        @pl.when(c + ring - ONE < nchunk)
        def _():
            fetch(c + ring - ONE)

        slot = c % ring
        pltpu.make_async_copy(d_hbm.at[pl.ds(ZERO, chunk)], buf.at[slot], sems.at[slot]).wait()

        def add(i, carry):
            acc[key_ref[c * chunk + i] % depth] += buf[slot, i]
            return carry

        lax.fori_loop(ZERO, chunk, add, ZERO, unroll=16)
        return carry

    lax.fori_loop(ZERO, nchunk, body, ZERO)
    sq = jnp.zeros((8, LANES), f32)
    for j in range(FOUR):
        done = ZERO
        for part, g_ref in enumerate(g_refs):
            take = min(g_ref.shape[ZERO], rows - done)
            cols = slice(j * LANES, (j + ONE) * LANES)
            val = own_refs[part][:take, cols] + g_ref[:take, cols] + acc[pl.ds(done, take), j, :]
            g_outs[j // TWO][done:done + take, (j % TWO) * LANES:(j % TWO + ONE) * LANES] = val
            sq = sq + jnp.sum((val * val).reshape(take // 8, 8, LANES), axis=ZERO)
            done += take
    sq_ref[:] = sq


def add_lookup_rows(count, keys, d_all, own, grads, rows, depth, chunk=64, ring=FOUR):
    vm = pl.BlockSpec(memory_space=pltpu.VMEM)
    sm = pl.BlockSpec(memory_space=pltpu.SMEM)
    dim = grads[ZERO].shape[ONE]
    return pl.pallas_call(
        functools.partial(scatter_kernel, chunk=chunk, depth=depth, ring=ring, nin=len(grads), rows=rows),
        in_specs=[sm, sm, pl.BlockSpec(memory_space=pl.ANY)] + [vm] * TWO * len(grads),
        out_specs=[vm, vm, vm],
        out_shape=[jax.ShapeDtypeStruct((rows, dim // TWO), f32), jax.ShapeDtypeStruct((rows, dim // TWO), f32), jax.ShapeDtypeStruct((8, LANES), f32)],
        scratch_shapes=[pltpu.VMEM((rows + 8, FOUR, LANES), f32), pltpu.VMEM((ring, chunk, FOUR, LANES), f32), pltpu.SemaphoreType.DMA((ring,))],
        compiler_params=pltpu.CompilerParams(vmem_limit_bytes=58 * MIB),
        cost_estimate=COST,
        name="lookup_rows")(count, keys, d_all, *own, *grads)


def small_sum_kernel(x_ref, o_ref, slots, send_sem, recv_sem, *, ntp, ndp):
    tp, dp = lax.axis_index('tp'), lax.axis_index('dp')
    me = tp * ndp + dp
    n = ntp * ndp
    barrier = pltpu.get_barrier_semaphore()
    peers = [(lax.rem(tp + k // ndp, ntp), lax.rem(dp + k % ndp, ndp)) for k in range(ONE, n)]
    for peer in peers:
        pl.semaphore_signal(barrier, inc=ONE, device_id=peer, device_id_type=MESH)
    pl.semaphore_wait(barrier, n - ONE)
    copies = []
    for k, peer in enumerate(peers):
        copies.append(pltpu.make_async_remote_copy(src_ref=x_ref, dst_ref=slots.at[me], send_sem=send_sem.at[k], recv_sem=recv_sem.at[k], device_id=peer, device_id_type=MESH))
        copies[-ONE].start()
    slots[me] = x_ref[:]
    for copy in copies:
        copy.wait()
    total = slots[ZERO]
    for k in range(ONE, n):
        total = total + slots[k]
    o_ref[:] = total


def small_sum(x, ntp, ndp, cid):
    vm = pl.BlockSpec(memory_space=pltpu.VMEM)
    n = ntp * ndp
    return pl.pallas_call(
        functools.partial(small_sum_kernel, ntp=ntp, ndp=ndp), in_specs=[vm], out_specs=vm,
        out_shape=jax.ShapeDtypeStruct(x.shape, f32),
        scratch_shapes=[pltpu.VMEM((n,) + x.shape, f32), pltpu.SemaphoreType.DMA((n - ONE,)), pltpu.SemaphoreType.DMA((n - ONE,))],
        compiler_params=pltpu.CompilerParams(collective_id=cid, has_side_effects=True),
        cost_estimate=COST)(x)


def grad_sum_kernel(*refs, nl, third, ntp, ndp, live, tt, sub, inv, row0):
    packs, x_ref, slab_ref, h_ref, lse_ref, lab_ref = refs[:nl], *refs[nl:nl + 5]
    out, small_out, g_ref, acc, r_core, r_one, r_two, r_last, slots, s_own, s_core, r_core_s, s_ring, r_ring, s_small, r_small, e_ref, s_slab = refs[nl + 5:]
    tp, dp = lax.axis_index('tp'), lax.axis_index('dp')
    me, n = tp * ndp + dp, ntp * ndp
    core, xx, yy = lax.rem(dp, TWO), lax.rem(dp // TWO, TWO), dp // FOUR
    near = {'core': (tp, dp + ONE - TWO * core), 'x': (tp, dp + TWO - FOUR * xx), 'y': (tp, dp + FOUR - 8 * yy), 'z': (ONE - tp, dp)}
    bit = {'x': xx, 'y': yy, 'z': tp}
    barrier = pltpu.get_barrier_semaphore()
    peers = [(lax.rem(tp + k // ndp, ntp), lax.rem(dp + k % ndp, ndp)) for k in range(ONE, n)]
    for peer in peers:
        pl.semaphore_signal(barrier, inc=ONE, device_id=peer, device_id_type=MESH)
    pl.semaphore_wait(barrier, n - ONE)

    def remote(src, dst, send, recv, peer):
        return pltpu.make_async_remote_copy(src_ref=src, dst_ref=dst, send_sem=send, recv_sem=recv, device_id=peer, device_id_type=MESH)

    over_core, own, small = {}, {}, []
    for k in range(THREE):
        for la in range(nl):
            rows = pl.ds(k * third, third)
            over_core[k, la] = remote(packs[la].at[:, ONE - core, rows, :], r_core.at[k, la], s_core.at[k, la], r_core_s.at[k, la], near['core'])
            over_core[k, la].start()
            own[k, la] = pltpu.make_async_copy(packs[la].at[:, core, rows, :], acc.at[k, la], s_own.at[k, la])
            own[k, la].start()
    for k, peer in enumerate(peers):
        small.append(remote(x_ref, slots.at[me], s_small.at[k], r_small.at[k], peer))
        small[-ONE].start()
    slots[me] = x_ref[:]

    orders = ('xyz', 'yzx', 'zxy')

    def block(fixed, free):
        val = dict(fixed)
        val.update(free)
        return val['z'] * FOUR + val['y'] * TWO + val['x']

    slab_copy = pltpu.make_async_copy(slab_ref.at[pl.ds(row0, e_ref.shape[ZERO])], e_ref, s_slab)
    slab_copy.start()
    base = (tp * ndp + dp) * live + row0
    ntok = h_ref.shape[ZERO] // tt
    nrow = e_ref.shape[ZERO] // sub

    def tile(i, carry):
        at = pl.multiple_of((i % nrow) * sub, sub)
        t = i // nrow
        h = h_ref[pl.ds(pl.multiple_of(t * tt, tt), tt), :]
        row = lax.broadcasted_iota(jnp.int32, (sub, ONE), ZERO) + (base + at)
        p = jnp.exp(dot(e_ref[pl.ds(at, sub), :], h, NT) - lse_ref[t])
        d = jnp.where(row == lab_ref[t], p - 1.0, p).astype(bf16)
        g_ref[pl.ds(at, sub), :] += dot(d, h, NN)
        return carry

    def head_rows(first, last):
        lax.fori_loop(first * ntok * nrow // 16, last * ntok * nrow // 16, tile, ZERO)

    recvs = (r_one, r_two, r_last)
    flight = {}

    def send(k, step):
        order = orders[k]
        fixed = {d: bit[d] for d in order[:step]}
        fixed[order[step]] = ONE - bit[order[step]]
        rest = order[step + ONE:]
        for la in range(nl):
            for i in range(TWO ** len(rest)):
                free = {d: (i >> j) % TWO for j, d in enumerate(rest)}
                c = remote(acc.at[k, la, block(fixed, free)], recvs[step].at[k, la, i], s_ring.at[step, k, la, i], r_ring.at[step, k, la, i], near[order[step]])
                c.start()
                flight[k, step, la, i] = c

    def take(k, step):
        order = orders[k]
        fixed = {d: bit[d] for d in order[:step + ONE]}
        rest = order[step + ONE:]
        for la in range(nl):
            for i in range(TWO ** len(rest)):
                flight[k, step, la, i].wait_recv()
                free = {d: (i >> j) % TWO for j, d in enumerate(rest)}
                at = block(fixed, free)
                acc[k, la, at] = acc[k, la, at] + recvs[step][k, la, i]

    g_ref[:] = jnp.zeros_like(g_ref)
    slab_copy.wait()
    head_rows(ZERO, FOUR)
    for k in range(THREE):
        for la in range(nl):
            own[k, la].wait()
            over_core[k, la].wait_recv()
            acc[k, la] = acc[k, la] + r_core[k, la]
        if k:
            send(k - ONE, ZERO)
    send(TWO, ZERO)
    head_rows(FOUR, 12)
    for step in range(ONE, THREE):
        for k in range(THREE):
            take(k, step - ONE)
            if k:
                send(k - ONE, step)
        send(TWO, step)
        head_rows(FOUR * step + 8, 16)
    g_ref[:] *= inv
    for k in range(THREE):
        take(k, TWO)
        at = block(bit, {})
        for la in range(nl):
            out[la, k * third:(k + ONE) * third, :] = acc[k, la, at]
    for c in list(over_core.values()) + list(flight.values()):
        c.wait_send()
    for c in small:
        c.wait()
    total = slots[ZERO]
    for k in range(ONE, n):
        total = total + slots[k]
    small_out[:] = total


def grad_sum(packs, x, slab, row0, nrow, h, lse, lab, live, inv, ntp, ndp, cid):
    nl, rows = len(packs), packs[ZERO].shape[TWO]
    dim = slab.shape[ONE]
    third = rows // THREE
    vm, hbm = pl.BlockSpec(memory_space=pltpu.VMEM), pl.BlockSpec(memory_space=pl.ANY)
    n = ntp * ndp
    dma, buf = pltpu.SemaphoreType.DMA, pltpu.VMEM
    return pl.pallas_call(
        functools.partial(grad_sum_kernel, nl=nl, third=third, ntp=ntp, ndp=ndp, live=live, tt=lse.shape[TWO], sub=nrow // 5, inv=inv, row0=row0),
        in_specs=[hbm] * nl + [vm, hbm, vm, vm, vm], out_specs=[vm, vm, vm],
        out_shape=[jax.ShapeDtypeStruct((nl, rows, WIDE), f32), jax.ShapeDtypeStruct(x.shape, f32), jax.ShapeDtypeStruct((nrow, dim), f32)],
        scratch_shapes=[buf((THREE, nl, 8, third, WIDE), f32), buf((THREE, nl, 8, third, WIDE), f32), buf((THREE, nl, FOUR, third, WIDE), f32),
                        buf((THREE, nl, TWO, third, WIDE), f32), buf((THREE, nl, ONE, third, WIDE), f32), buf((n,) + x.shape, f32),
                        dma((THREE, nl)), dma((THREE, nl)), dma((THREE, nl)), dma((THREE, THREE, nl, FOUR)), dma((THREE, THREE, nl, FOUR)), dma((n - ONE,)), dma((n - ONE,)), buf((nrow, dim), bf16), dma],
        compiler_params=pltpu.CompilerParams(collective_id=cid, has_side_effects=True, vmem_limit_bytes=63 * MIB),
        cost_estimate=COST)(*packs, x, slab, h, lse, lab)


def adam_kernel(where_ref, clip_ref, tok_ref, *refs, n):
    g_refs, (p_ref, m_ref, v_ref), (po, mo, vo, bo, tok) = refs[:n], refs[n:n + THREE], refs[-5:]
    for k in range(n):
        @pl.when(pl.program_id(ZERO) == k)
        def _(k=k):
            new, mom, vel = adam_update(p_ref[:], g_refs[k][:] * clip_ref[ZERO], m_ref[:], v_ref[:], True)
            tok[:] = new[:8, :LANES]
            po[:] = new
            mo[:] = mom
            vo[:] = vel
            bo[:] = new.astype(bf16)


def adam_rows(where, clip, tok, grads, master, mom, vel, prev, nblk):
    n, (rows, wide) = len(grads), grads[ZERO].shape
    r = rows // nblk
    blk = pl.BlockSpec((r, wide), lambda i, j, w: (w[ZERO, i] + j, w[ONE, i]))
    anyspec = pl.BlockSpec(memory_space=pl.ANY)
    ins = [where, clip, tok] + list(grads) + [master, mom, vel]
    hold = lambda k: (lambda i, j, w: (jnp.where(i == k, j, jnp.where(i < k, ZERO, nblk - ONE)), ZERO))
    in_specs = [pl.BlockSpec(memory_space=pltpu.SMEM), anyspec] + [pl.BlockSpec((r, wide), hold(k)) for k in range(n)] + [blk] * THREE
    aliases = {}
    if prev is not None:
        aliases = {len(ins) + i: i for i in range(FOUR)}
        ins += list(prev)
        in_specs += [anyspec] * FOUR
    full = jax.ShapeDtypeStruct(master.shape, f32)
    return pl.pallas_call(
        functools.partial(adam_kernel, n=n),
        grid_spec=pltpu.PrefetchScalarGridSpec(num_scalar_prefetch=ONE, grid=(n, nblk), in_specs=in_specs, out_specs=[blk] * FOUR + [pl.BlockSpec((8, LANES), lambda i, j, w: (ZERO, ZERO))]),
        out_shape=[full, full, full, jax.ShapeDtypeStruct(master.shape, bf16), jax.ShapeDtypeStruct((8, LANES), f32)],
        input_output_aliases=aliases,
        compiler_params=pltpu.CompilerParams(dimension_semantics=("arbitrary", "arbitrary"), vmem_limit_bytes=48 * MIB),
        cost_estimate=COST,
        name="adam_rows")(*ins)


def solution(mesh):
    ntp, ndp = mesh.shape['tp'], mesh.shape['dp']
    ndev = ntp * ndp
    SWAP = {'z': [(i, ONE - i) for i in range(TWO)], 'core': [(i, i ^ ONE) for i in range(ndp)], 'x': [(i, i ^ TWO) for i in range(ndp)], 'y': [(i, i ^ FOUR) for i in range(ndp)]}

    def swap_on(val, axis):
        if axis == 'xz':
            return lax.ppermute(val, ('tp', 'dp'), [(i, i ^ (ndp + TWO)) for i in range(ndev)])
        return lax.ppermute(val, 'tp' if axis == 'z' else 'dp', SWAP[axis])

    def device_step(tokens, labels, *state):
        masters, moms, vels = state[ZERO:8], state[8:16], state[16:24]
        embedding, vec_params, w_qkv, b_qkv, w_out, w_up, b_up, w_down = masters
        z, dp = lax.axis_index('tp'), lax.axis_index('dp')
        yb, xb, cb = dp // FOUR, (dp // TWO) % TWO, dp % TWO
        vocab_loc, dim = embedding.shape
        layers = w_qkv.shape[ZERO]
        seq = tokens.shape[ONE]
        heads_loc, hd = b_qkv.shape[ONE], b_qkv.shape[TWO] // THREE
        heads = heads_loc * ntp
        n_total = seq * ndev
        vocab_base = z * vocab_loc
        live = vocab_loc // ndp
        half = -(-live // LANES) * LANES
        pick = lambda arr, i: lax.dynamic_index_in_dim(arr, i, ZERO, keepdims=False)

        def rows_of(ids):
            local = ids - vocab_base
            ok = (local >= ZERO) & (local < vocab_loc)
            return jnp.where(ok[:, None], gather_rows(jnp.where(ok, local, jnp.where(local < ZERO, local + vocab_loc, local - vocab_loc)), embedding), 0.0)

        tok_own, tok_oth = pick(tokens, z), pick(tokens, ONE - z)
        lab_own, lab_oth = pick(labels, z), pick(labels, ONE - z)
        ws = (w_down, w_up, w_out, w_qkv)
        dp1 = dp.reshape(ONE)
        got = [swap_on(pack_share(dp1, ws, layer, ndp), 'z') for layer in range(layers)]
        rows_out = rows_of(tok_oth)
        other = [lax.all_gather(g, 'dp', axis=ZERO, tiled=False) for g in got]
        row_got = swap_on(rows_out, 'z')
        row_own = rows_of(tok_own)
        lab_oth_rows, lab_own_rows = rows_of(lab_oth), rows_of(lab_own)
        bias_oth = swap_on(jnp.concatenate([b_qkv.reshape(layers, -ONE), b_up], axis=ONE), 'z')
        slab = make_slab(jnp.stack([dp, dp ^ FOUR]), embedding, live, half)

        ids = jnp.stack([jnp.stack([tok_own, tok_oth]), jnp.stack([lab_own, lab_oth])])
        ids = jnp.stack([ids, swap_on(ids, 'core')])
        ids = jnp.stack([ids, swap_on(ids, 'x')])
        ids_y = jnp.stack([ids, swap_on(ids, 'y')])
        tok_all = ids_y[:, :, :, ZERO]
        for axis, bit in ((ZERO, yb), (ONE, xb), (TWO, cb), (THREE, z)):
            tok_all = jnp.where(bit == ONE, jnp.flip(tok_all, axis), tok_all)
        tok_all = jnp.transpose(tok_all, (THREE, ZERO, ONE, TWO, FOUR)).reshape(-ONE)
        depth = ONE << (live - ONE).bit_length()
        row_id = tok_all - (vocab_base + dp * live)
        mine = (row_id >= ZERO) & (row_id < live)
        key = jnp.where(mine, jnp.arange(tok_all.shape[ZERO], dtype=jnp.int32) * depth + row_id, jnp.iinfo(jnp.int32).max)
        key = lax.sort(key, is_stable=False)
        key = jnp.where(key == jnp.iinfo(jnp.int32).max, live, key)
        count = jnp.sum(mine.astype(jnp.int32)).reshape(ONE)

        early = (row_own, lab_oth_rows, lab_own_rows, slab, key, count, ids, bias_oth, other[ZERO])
        row_own, lab_oth_rows, lab_own_rows, slab, key, count, ids, bias_oth, other[ZERO] = lax.optimization_barrier(early)
        joined = [join_halves(other[ZERO], ws, ZERO, hd)]
        row_got, joined[ZERO] = lax.optimization_barrier((row_got, joined[ZERO]))
        x_embed = row_got + row_own
        x_label = swap_on(lab_oth_rows, 'z') + lab_own_rows

        nbq = heads_loc * THREE * hd
        by_kind = lambda w: w.reshape(w.shape[:-ONE] + (heads_loc, THREE, hd)).swapaxes(-THREE, -TWO).reshape(w.shape[:-ONE] + (THREE, heads_loc * hd))

        def biases(layer):
            bq = jnp.concatenate([by_kind(b_qkv[layer].reshape(-ONE)), by_kind(bias_oth[layer, :nbq])], axis=-ONE).reshape(-ONE)
            return bq, jnp.concatenate([b_up[layer], bias_oth[layer, nbq:]], axis=ZERO)

        weights = []
        slope_all = jnp.array(alibi_slopes(heads), dtype=f32).reshape(ntp, heads_loc)
        slopes = jnp.concatenate([pick(slope_all, z), pick(slope_all, ONE - z)])

        ablk = min(512, seq)
        resid, ln_zero_vjp = jax.vjp(layer_norm, x_embed, vec_params[ZERO], vec_params[ONE])
        saved = []
        for layer in range(layers):
            k = TWO + 6 * layer
            wd, wu, wo, wq = joined[layer]
            bq, bu = biases(layer)
            weights.append((wq, bq, wo, wu, bu, wd))
            normed_one, ln_one_vjp = jax.vjp(layer_norm, resid, vec_params[k], vec_params[k + ONE])
            act_in = normed_one.astype(bf16)
            qkv = (dot(act_in, wq, NN) + bq).astype(bf16)
            context = attn_fwd(qkv, slopes, hd, ablk)
            if layer + ONE < layers:
                context, other[layer + ONE] = lax.optimization_barrier((context, other[layer + ONE]))
                joined.append(join_halves(other[layer + ONE], ws, layer + ONE, hd))
            mid = resid + (dot(context, wo, NN) + vec_params[k + TWO])
            normed_two, ln_two_vjp = jax.vjp(layer_norm, mid, vec_params[k + THREE], vec_params[k + FOUR])
            mlp_in = normed_two.astype(bf16)
            act_out, gelu_vjp = jax.vjp(gelu_tanh, dot(mlp_in, wu, NN) + bu)
            hidden = act_out.astype(bf16)
            resid = mid + dot(hidden, wd, NN) + vec_params[k + 5]
            saved.append((ln_one_vjp, act_in, qkv, context, ln_two_vjp, mlp_in, gelu_vjp, hidden))

        fin = TWO + 6 * layers
        normed_fin, ln_fin_vjp = jax.vjp(layer_norm, resid, vec_params[fin], vec_params[fin + ONE])
        t = seq // TWO
        core_own = swap_on(normed_fin, 'core')
        first, core_own = lax.optimization_barrier((normed_fin, core_own))
        a_own, b_own = first[:t], first[t:]
        a_x, a_z = swap_on(a_own, 'x'), swap_on(a_own, 'z')
        b_x, b_z = swap_on(b_own, 'x'), swap_on(b_own, 'z')
        groups = [[(first, ZERO), (first, ONE)], [(a_x, ZERO), (a_z, ZERO)], [(b_x, ZERO), (b_z, ZERO)], None, []]
        masks = [[(ZERO, ZERO, ZERO), (ZERO, ZERO, ONE)], [(ONE, ZERO, ZERO), (ZERO, ONE, ZERO)], [(ONE, ZERO, ONE), (ZERO, ONE, ONE)], [(ONE, ONE, ZERO), (ONE, ONE, ONE)]]
        hb, pos, self_sum, core_sum, tops, totals = None, ZERO, [], [], [], []
        from_core = []
        where_piece = {}
        for i, group in enumerate(groups):
            res = head_fwd(slab, group, from_core, hb, pos, 16, t, live, 1280)
            hb, top, total = res[-ONE], res[-THREE], res[-TWO]
            if i == ONE:
                a_far, b_far, top = lax.optimization_barrier((a_own, b_own, top))
                groups[THREE] = [(swap_on(a_far, 'xz'), ZERO), (swap_on(b_far, 'xz'), ZERO)]
            tops.append(top)
            totals.append(total)
            for side, names in ((ZERO, masks[i] if group else ()), (ONE, masks[i - ONE] if from_core else ())):
                for nm in names:
                    where_piece[nm + (side,)] = pos
                    pos += ONE
            if group:
                self_sum.append(res[ZERO])
            if from_core:
                core_sum.append(swap_on(res[-FOUR], 'core'))
            if i == ZERO:
                from_core = [(core_own, ZERO), (core_own, ONE)]
            elif group:
                moved = [arr for arr, _ in group]
                *moved, tops[i - ONE] = lax.optimization_barrier((*moved, tops[i - ONE]))
                from_core = [(swap_on(arr, 'core'), ZERO) for arr in moved]
        cube = [(x, zz, c, h) for x in range(TWO) for zz in range(TWO) for c in range(TWO) for h in range(TWO)]
        back = [ZERO] * 16
        for i, (x, zz, c, h) in enumerate(cube):
            back[where_piece[(x, zz, h, c)]] = i
        to_cube = lambda v: jnp.stack([v[where_piece[(x, zz, h, c)]] for x, zz, c, h in cube])
        from_cube = lambda v: jnp.stack([v[back[i]] for i in range(16)])
        m_loc = jnp.concatenate(tops).reshape(16, t)
        s_loc = jnp.concatenate(totals).reshape(16, t)
        stat = jnp.stack([to_cube(m_loc), to_cube(s_loc)]).reshape(TWO, TWO, TWO, TWO, TWO, t)
        m_core = None
        for axis, name in ((THREE, 'core'), (ONE, 'x'), (TWO, 'z')):
            got = jnp.flip(swap_on(stat, name), axis)
            if m_core is None:
                m_core = from_cube(got[ZERO].reshape(16, t))
            top = jnp.maximum(stat[ZERO], got[ZERO])
            stat = jnp.stack([top, stat[ONE] * jnp.exp(stat[ZERO] - top) + got[ONE] * jnp.exp(got[ZERO] - top)])
        stat = stat.reshape(TWO, 16, t)
        lse_cube = stat[ZERO] + jnp.log(stat[ONE])
        lse = from_cube(lse_cube)
        lab = from_cube(jnp.transpose(ids[:, :, ONE], (ZERO, TWO, ONE, THREE)).reshape(16, t))

        inv_n = 1.0 / n_total
        w_self, w_core = jnp.exp(m_loc - lse) * inv_n, jnp.exp(m_core - lse) * inv_n
        spread = lambda w, names, side: jnp.concatenate([w[where_piece[nm + (side,)]] for nm in names]).reshape(-ONE, ONE)
        reduced = [mine * spread(w_self, names, ZERO) + theirs * spread(w_core, names, ZERO) for mine, theirs, names in zip(self_sum, core_sum, masks)]
        r_own, r_one, r_two, r_far = reduced

        tt = 2048
        lse_t, lab_t = lse.reshape(-ONE, ONE, tt), lab.reshape(-ONE, ONE, tt)
        vb = half // TWO
        grad_args = dict(vb=vb, tt=tt, sub=vb // 5, inv=inv_n)
        base_own = (vocab_base + dp * live).reshape(ONE)
        base_oth = (vocab_base + (dp ^ FOUR) * live).reshape(ONE)
        hb0, r_own, r_one, r_two, r_far = lax.optimization_barrier((hb, r_own, r_one, r_two, r_far))
        got_z, got_far_z = swap_on(r_one[t:], 'z'), swap_on(r_far[:t], 'z')
        got_x, got_far_x = swap_on(r_two[:t], 'x'), swap_on(r_far[t:], 'x')
        g_send = head_grad(base_oth, slab, TWO, ONE, hb0, lse_t, lab_t, **grad_args)
        g_sent = [swap_on(g_send, 'y')]
        hb1, g_send, got_z, got_far_z, got_x, got_far_x = lax.optimization_barrier((hb0, g_send, got_z, got_far_z, got_x, got_far_x))
        a_sum, a_x_sum = r_own[:t] + got_z, r_one[:t] + got_far_z
        b_sum, b_z_sum = r_own[t:] + got_x, r_two[t:] + got_far_x
        hb1, a_x_sum, b_z_sum = lax.optimization_barrier((hb1, a_x_sum, b_z_sum))
        a_last, b_last = swap_on(a_x_sum, 'x'), swap_on(b_z_sum, 'z')
        g_send = head_grad(base_oth + vb, slab, THREE, ONE, hb1, lse_t, lab_t, **grad_args)
        g_sent.append(swap_on(g_send, 'y'))
        a_last, b_last, x_label = lax.optimization_barrier((a_last, b_last, x_label))
        d_head = jnp.concatenate([a_sum + a_last, b_sum + b_last], axis=ZERO) - x_label * inv_n
        target = jnp.sum(normed_fin.astype(bf16).astype(f32) * x_label, axis=ONE)
        loss_sum = jnp.sum(lse_cube[ZERO:TWO].reshape(-ONE) - target)

        vec_grads = {}
        d_resid, vec_grads[fin], vec_grads[fin + ONE] = ln_fin_vjp(d_head)
        bias_grads, part = {}, {}
        z1 = z.reshape(ONE)
        to_heads = lambda g: g.reshape(THREE, heads_loc, hd).swapaxes(ZERO, ONE).reshape(-ONE)
        rows_mlp = (w_down.shape[ONE] * w_down.shape[TWO] + w_up.shape[ONE] * w_up.shape[TWO]) // (ndp * WIDE)
        rows_attn = (w_out.shape[ONE] * w_out.shape[TWO] + w_qkv.shape[ONE] * w_qkv.shape[TWO]) // (ndp * WIDE)
        narrow = tt // TWO

        def sum_layer(layer, x, h, cid):
            pack = part[layer].reshape(ndev // TWO, TWO, -ONE, WIDE)
            return grad_sum([pack], x, slab, layer * vb, vb, h, lse.reshape(-ONE, ONE, narrow), lab.reshape(-ONE, ONE, narrow), live, inv_n, ntp, ndp, cid)

        for layer in reversed(range(layers)):
            ln_one_vjp, act_in, qkv, context, ln_two_vjp, mlp_in, gelu_vjp, hidden = saved[layer]
            wq, bq, wo, wu, bu, wd = weights[layer]
            k = TWO + 6 * layer
            vec_grads[k + 5] = jnp.sum(d_resid, axis=ZERO)
            d_out = d_resid.astype(bf16)
            d_pre = gelu_vjp(dot(d_out, wd, NT))[ZERO]
            g_bup = jnp.sum(d_pre, axis=ZERO)
            d_pre_b = d_pre.astype(bf16)
            g_pack = wgrad(wgrad_mlp_kernel, z1, (ONE, ZERO, ZERO, ONE), (hidden, d_out, mlp_in, d_pre_b), ndp, rows_mlp, ZERO, rows_mlp + rows_attn, None)
            d_mid_ln, vec_grads[k + THREE], vec_grads[k + FOUR] = ln_two_vjp(dot(d_pre_b, wu, NT))
            d_mid = d_resid + d_mid_ln
            vec_grads[k + TWO] = jnp.sum(d_mid, axis=ZERO)
            d_attn = d_mid.astype(bf16)
            d_context = dot(d_attn, wo, NT).astype(bf16)
            d_q, d_k, d_v, d_b = attn_bwd(qkv, d_context, slopes, hd, ablk)
            d_q, g_sent[layers - ONE - layer] = lax.optimization_barrier((d_q, g_sent[layers - ONE - layer]))
            d_res_ln, vec_grads[k], vec_grads[k + ONE] = ln_one_vjp(dot(jnp.concatenate([d_q, d_k, d_v], axis=ONE), wq, NT))
            d_resid = d_mid + d_res_ln
            if layer == ZERO:
                d_embed, vec_grads[ZERO], vec_grads[ONE] = ln_zero_vjp(d_resid)
                d_embed, hb2 = lax.optimization_barrier((d_embed, hb1))
                d_all = lax.all_gather(d_embed.reshape(seq, dim // LANES, LANES), ('tp', 'dp'), axis=ZERO, tiled=True)
            part[layer] = wgrad(wgrad_attn_kernel, z1, (ONE, ZERO, ZERO, ONE, ONE, ONE), (context, d_attn, act_in, d_q, d_k, d_v), ndp, rows_attn, rows_mlp, rows_mlp + rows_attn, g_pack)
            if layer == ONE:
                piece_1, _, own_1 = sum_layer(ONE, jnp.zeros((8, LANES), f32), hb1, THREE)
                d_resid, piece_1 = lax.optimization_barrier((d_resid, piece_1))
            d_bias = d_b[:THREE].reshape(THREE, ntp, heads_loc * hd)
            bias_grads[layer] = (to_heads(d_bias[:, ZERO]), to_heads(d_bias[:, ONE]), g_bup[:b_up.shape[ONE]], g_bup[b_up.shape[ONE]:])

        vec_g = jnp.stack([vec_grads[row] for row in range(fin + TWO)])
        own_b = jnp.concatenate([jnp.concatenate([bias_grads[la][ZERO], bias_grads[la][TWO]]) for la in range(layers)])
        oth_b = jnp.concatenate([jnp.concatenate([bias_grads[la][ONE], bias_grads[la][THREE]]) for la in range(layers)])
        both = jnp.where(z == ZERO, jnp.stack([own_b, oth_b]), jnp.stack([oth_b, own_b]))
        small = jnp.concatenate([vec_g.reshape(-ONE), both.reshape(-ONE), jnp.full((1024,), 1.0 / 1024, f32) * loss_sum])
        piece_0, small, own_0 = sum_layer(ZERO, small.reshape(-ONE, LANES), hb2, ONE)
        pieces = jnp.concatenate([piece_0, piece_1], axis=ZERO)
        small, pieces = small.reshape(-ONE), pieces.reshape(-ONE, WIDE)
        d_all, pieces = lax.optimization_barrier((d_all, pieces))
        left, right, sq_emb = add_lookup_rows(count, key, d_all, [own_0, own_1], g_sent, live, depth)
        nvec, nb = vec_g.size, own_b.size
        g_vec = small[:nvec].reshape(vec_g.shape)
        b_all = small[nvec:nvec + TWO * nb].reshape(TWO, nb)
        g_bias = pick(b_all, z).reshape(layers, -ONE)
        loss = jnp.sum(small[nvec + TWO * nb:]) / n_total
        sq_small = jnp.sum(g_vec * g_vec) + jnp.sum(b_all * b_all)

        sq_here = jnp.sum(sq_emb) + jnp.sum(pieces * pieces)
        sq_total = small_sum(jnp.full((8, LANES), 1.0 / 1024, f32) * sq_here, ntp, ndp, TWO)
        clip_coef = jnp.minimum(1.0, CLIP_NORM / (jnp.sqrt(jnp.sum(sq_total) + sq_small) + 1e-6))

        g_layers = lax.all_gather(pieces, 'dp', axis=ZERO, tiled=False)
        order = (7, 5, FOUR, TWO)
        take = lambda st: [st[i] for i in order]
        res = adam_layers(clip_coef.reshape(ONE), g_layers, take(masters), take(moms), take(vels), layers, hd)
        g_bqkv = g_bias[:, :nbq].reshape(b_qkv.shape)
        small_grads = {ONE: g_vec, THREE: g_bqkv, 6: g_bias[:, nbq:]}

        left, right, clip_coef = lax.optimization_barrier((left, right, clip_coef))
        left_x, right_y = swap_on(left, 'x'), swap_on(right, 'y')
        left_y, right_x = swap_on(left, 'y'), swap_on(right, 'x')
        nblk, emb_new, clip1 = THREE, None, clip_coef.reshape(ONE)
        tok = jnp.zeros((8, LANES), f32)

        def update(pieces, prev, tok, first=ZERO, count=nblk):
            where = jnp.stack([jnp.stack([(dp ^ mask) * nblk + first for _, mask, _ in pieces]), jnp.array([col for _, _, col in pieces], jnp.int32)])
            *new, tok = adam_rows(where, clip1, tok, [g for g, _, _ in pieces], embedding, moms[ZERO], vels[ZERO], prev, count)
            return new, tok

        over = lambda pieces: [(swap_on(g, 'core'), mask + ONE, col) for g, mask, col in pieces]
        stage = [(left, ZERO, ZERO), (right, ZERO, ONE)]
        cross = over(stage)
        emb_new, tok = update(stage, None, tok)
        emb_new, tok = update(cross, emb_new, tok)
        left_x, right_y, tok = lax.optimization_barrier((left_x, right_y, tok))
        r = live // nblk
        far = [(swap_on(left_x[j * r:(j + ONE) * r], 'y'), swap_on(right_y[j * r:(j + ONE) * r], 'x')) for j in range(nblk)]
        stages = [([(left_x, TWO, ZERO), (right_y, FOUR, ONE)], ZERO, nblk), ([(left_y, FOUR, ZERO), (right_x, TWO, ONE)], ZERO, nblk)]
        stages += [([(fl, 6, ZERO), (fr, 6, ONE)], j, ONE) for j, (fl, fr) in enumerate(far)]
        for stage, first_blk, nb_here in stages:
            *got, tok = lax.optimization_barrier((*(g for g, _, _ in stage), tok))
            stage = [(g, mask, col) for g, (_, mask, col) in zip(got, stage)]
            cross = over(stage)
            emb_new, tok = update(stage, emb_new, tok, first_blk, nb_here)
            emb_new, tok = update(cross, emb_new, tok, first_blk, nb_here)

        updated = {ZERO: tuple(emb_new)}
        for i, slot in enumerate(order):
            updated[slot] = (res[i], res[FOUR + i], res[8 + i], res[12 + i])
        for slot, g in small_grads.items():
            new = adam_update(masters[slot], g * clip_coef, moms[slot], vels[slot], DECAYED[slot])
            updated[slot] = (*new, new[ZERO].astype(bf16))
        new_masters, new_moms, new_vels, new_bf16 = ([updated[slot][i] for slot in range(8)] for i in range(FOUR))
        return (loss, *new_masters, *new_moms, *new_vels, *new_bf16)

    data_spec = P('dp', None)
    return jax.shard_map(device_step, mesh=mesh, in_specs=(data_spec, data_spec) + PARAM_SPECS * THREE, out_specs=(P(),) + PARAM_SPECS * FOUR, check_vma=False)
```

time: 2930 us -> 1330 us (0.45)
  waiting for transfers between devices: 1590 us -> 248 us
  Pallas kernels: 0 us -> 786 us
  matrix products: 612 us -> 55.6 us
  other arithmetic: 537 us -> 78.9 us
  starting transfers between devices: 0.98 us -> 46.6 us
  blocking collectives: 43.9 us -> 0 us
  local copies, waits for them, and re-layouts: 116 us -> 80.1 us
    psum x11 -> x0, waiting for transfers between devices: 1590 us -> none  [the longest x1 685 us: device_step(): grads = [lax.psum(grad_arr, 'dp') for grad_arr in grads]]
    pallas_call x0 -> x41, Pallas kernels: none -> 786 us  [the longest x2 189 us: grad_sum(): pl.pallas_call(functools.partial(grad_sum_kernel, nl=nl, third=third, ntp...]
    dot_general x37 -> x16, matrix products: 567 us -> 55.6 us  [dot(): return lax.dot_general(a, b, dims, preferred_element_type=f32)]
    convert_element_type x17 -> x10, other arithmetic: 294 us -> 8.04 us  [the longest x2 3.2 us: device_step(): act_in = normed_one.astype(bf16)]
    ppermute x0 -> x58, waiting for transfers between devices: none -> 206 us  [the longest x56 200 us: swap_on(): return lax.ppermute(val, 'tp' if axis == 'z' else 'dp', SWAP[axis])]
    reduce_sum x33 -> x24, other arithmetic: 142 us -> 21.8 us  [the longest x8 10.5 us: layer_norm(): centred = values - jnp.mean(values, axis=-ONE, keepdims=True)]
    scatter-add x1 -> x0, other arithmetic: 46.4 us -> none  [local_grads(): jax.ops.segment_sum(d_rows, safe_ids, num_segments=vocab_loc)]
    ppermute x0 -> x58, starting transfers between devices: none -> 46.4 us  [the longest x56 43.5 us: swap_on(): return lax.ppermute(val, 'tp' if axis == 'z' else 'dp', SWAP[axis])]
  transfers between devices with their start and end apart: 11 -> 62, of which waited for: 11 -> 20; matrix products, arithmetic and copies ran while one was open for 5% -> 9% of each run, Pallas kernels for 0% -> 56%
where the time goes in v1:
time: 1330 us; the launch traced here: 1320 us
  Pallas kernels  786 us (59%)
  waiting for transfers between devices  248 us (19%)
  local copies, waits for them, and re-layouts  80.1 us (6%)
  other arithmetic  78.9 us (6%)
  matrix products  55.6 us (4%)
  starting transfers between devices  46.6 us (4%)
  between operations  22.6 us (2%)
    ppermute x56, waiting for transfers between devices, swap_on(): return lax.ppermute(val, 'tp' if axis == 'z' else 'dp', SWAP[axis])  200 us
    pallas_call x2, Pallas kernels, grad_sum(): pl.pallas_call(functools.partial(grad_sum_kernel, nl=nl, third=third, ntp...  189 us
    pallas_call x5, Pallas kernels, head_fwd(): pl.pallas_call(functools.partial(head_fwd_kernel, npiece=n, nself=k, vb=v...  153 us
    pallas_call x12, Pallas kernels, adam_rows(): pl.pallas_call(functools.partial(adam_kernel, n=n), grid_spec=pltpu.Prefe...  152 us
    pallas_call x2, Pallas kernels, head_grad(): pl.pallas_call(functools.partial(head_grad_kernel, tt=tt, sub=sub, inv=in...  69.1 us
    dot_general x16, matrix products, dot(): return lax.dot_general(a, b, dims, preferred_element_type=f32)  55.6 us
    unnamed x312, local copies, waits for them, and re-layouts  54.7 us
    pallas_call x2, Pallas kernels, attn_bwd(): pl.pallas_call(functools.partial(attn_bwd_kernel, blk=blk, hd=hd), grid=(...  50.6 us
  transfers between devices with their start and end apart: 62, of which 20 were waited for; matrix products, arithmetic and copies ran while one was open for 9% of the time, Pallas kernels for 56%

profile of v1, /device:TPU:0, one launch (start us, length us, event | category | flops | bytes accessed | tf_op | source)
XLA Modules:
  0.0 1317.7 jit_solution(14890352652297741480)
XLA Ops:
  9.3 3.3 collective-permute-start.5
  12.6 17.7 %collective-permute-done.5 = f32[768,256]{1,0:T(8,128)S(1)} collective-permute-done((f32[768,256]{1,0:T(8,128)}, f32[768,256]{1,0:T(8,128)S(1)}, u32[]{:S(2)}, u32[]{:S(2)}) %collective-permute-start.5) | collective-permute-done | bytes 786464 | tf_op jit(solution)/shard_map/ppermute | solution.py:758
  35.1 17.2 %collective-permute-done.6 = f32[768,256]{1,0:T(8,128)S(1)} collective-permute-done((f32[768,256]{1,0:T(8,128)}, f32[768,256]{1,0:T(8,128)S(1)}, u32[]{:S(2)}, u32[]{:S(2)}) %collective-permute-start.6) | collective-permute-done | bytes 786464 | tf_op jit(solution)/shard_map/ppermute | solution.py:758
  55.0 7.0 gather_rows.4
  64.1 7.0 gather_rows.7
  71.2 7.0 gather_rows.6
  78.2 6.9 gather_rows.5
  91.8 5.8 make_slab.1.refs_0_.e_ref.refs_2_
  102.3 4.3 collective-permute-done.3
  108.0 6.3 sort.7
  120.6 5.7 join_halves.2
  140.3 12.9 attn_fwd.2.ctx
  154.3 3.1 fusion.89
  159.7 6.0 multiply_convert_fusion.1
  171.8 5.7 join_halves.3
  187.2 12.9 attn_fwd.3.ctx
  203.5 6.0 multiply_convert_fusion
  213.3 4.3 collective-permute-done.7.refs_3_.refs_4_
  222.8 20.5 %head_fwd.5 = (f32[1024,512]{1,0:T(8,128)}, f32[2,1,512]{2,1,0:T(1,128)}, f32[2,1,512]{2,1,0:T(1,128)}, bf16[8192,512]{1,0:T(8,128)(2,1)}) custom-call(bf16[6400,512]{1,0:T(8,128)(2,1)} %copy-done, f32[1024,512]{1,0:T(8,128)} %copy-done.68, f32[1024,512]{1,0:T(8,128)} %copy-done.68), custom_call_target="tpu_custom_call" | custom-call | flops 1000000 | bytes 1000000 | tf_op jit(solution)/shard_map/head_fwd/pallas_call | solution.py:437
  246.0 37.5 %head_fwd.6 = (f32[1024,512]{1,0:T(8,128)}, f32[1024,512]{1,0:T(8,128)}, f32[4,1,512]{2,1,0:T(1,128)}, f32[4,1,512]{2,1,0:T(1,128)}, bf16[8192,512]{1,0:T(8,128)(2,1)}) custom-call(bf16[6400,512]{1,0:T(8,128)(2,1)} %copy-done, f32[512,512]{1,0:T(8,128)} %collective-permute-done.8.refs_1_, ...), custom_call_target="tpu_custom_call", output_to_operand_aliasing={{4}: (5, {})} | custom-call | flops 1000000 | bytes 1000000 | tf_op jit(solution)/shard_map/head_fwd/pallas_call | solution.py:437
  289.8 37.2 %head_fwd.7 = (f32[1024,512]{1,0:T(8,128)}, f32[1024,512]{1,0:T(8,128)}, f32[4,1,512]{2,1,0:T(1,128)}, f32[4,1,512]{2,1,0:T(1,128)}, bf16[8192,512]{1,0:T(8,128)(2,1)}) custom-call(bf16[6400,512]{1,0:T(8,128)(2,1)} %copy-done, f32[512,512]{1,0:T(8,128)} %copy-done.88, f32[512,512]{1,0:T(8,128)} %copy-done.89, ...), custom_call_target="tpu_custom_call", output_to_operand_aliasing={{4}: (5, {})} | custom-call | flops 1000000 | bytes 1000000 | tf_op jit(solution)/shard_map/head_fwd/pallas_call | solution.py:437
  327.0 6.3 collective-permute-done.11.refs_2_
  333.9 37.2 %head_fwd.8 = (f32[1024,512]{1,0:T(8,128)}, f32[1024,512]{1,0:T(8,128)}, f32[4,1,512]{2,1,0:T(1,128)}, f32[4,1,512]{2,1,0:T(1,128)}, bf16[8192,512]{1,0:T(8,128)(2,1)}) custom-call(bf16[6400,512]{1,0:T(8,128)(2,1)} %copy-done, f32[512,512]{1,0:T(8,128)} %copy-done.87, f32[512,512]{1,0:T(8,128)} %collective-permute-done.11.refs_2_, ...), custom_call_target="tpu_custom_call", output_to_operand_aliasing={{4}: (5, {})} | custom-call | flops 1000000 | bytes 1000000 | tf_op jit(solution)/shard_map/head_fwd/pallas_call | solution.py:437
  373.9 20.6 %head_fwd.9 = (f32[1024,512]{1,0:T(8,128)}, f32[2,1,512]{2,1,0:T(1,128)}, f32[2,1,512]{2,1,0:T(1,128)}, bf16[8192,512]{1,0:T(8,128)(2,1)}) custom-call(bf16[6400,512]{1,0:T(8,128)(2,1)} %copy-done, f32[512,512]{1,0:T(8,128)} %collective-permute-done.16.refs_1_, f32[512,512]{1,0:T(8,128)} %collective-permute-done.17.refs_2_, ...), custom_call_target="tpu_custom_call", output_to_operand_aliasing={{3}: (3, {})} | custom-call | flops 1000000 | bytes 1000000 | tf_op jit(solution)/shard_map/head_fwd/pallas_call | solution.py:437
  398.7 3.2 collective-permute-done.21
  406.7 4.1 multiply_add_fusion.3
  429.2 34.8 %head_grad.2 = f32[1600,512]{1,0:T(8,128)} custom-call(s32[1]{0:T(128)} %bitcast.98.base_ref, bf16[6400,512]{1,0:T(8,128)(2,1)} %copy-done, bf16[8192,512]{1,0:T(8,128)(2,1)} %get-tuple-element.318.h_ref.refs_3_, f32[4,1,2048]{2,1,0:T(1,128)} %reshape.537.lse_ref, s32[4,1,2048]{2,1,0:T(1,128)} %reshape.539.lab_ref), custom_call_target="tpu_custom_call" | custom-call | flops 1000000 | bytes 1000000 | tf_op jit(solution)/shard_map/head_grad/pallas_call | solution.py:469
  464.0 4.8 collective-permute-done.27
  475.8 38.0 %collective-permute-done.33 = f32[1024,512]{1,0:T(8,128)} collective-permute-done((f32[1024,512]{1,0:T(8,128)}, f32[1024,512]{1,0:T(8,128)}, u32[]{:S(2)}, u32[]{:S(2)}) %collective-permute-start.33) | collective-permute-done | bytes 2097184 | tf_op jit(solution)/shard_map/ppermute | solution.py:758
  513.7 4.0 add.485
  519.7 34.3 %head_grad.3 = f32[1600,512]{1,0:T(8,128)} custom-call(s32[1]{0:T(128)S(6)} %add.492.base_ref, bf16[6400,512]{1,0:T(8,128)(2,1)} %copy-done, bf16[8192,512]{1,0:T(8,128)(2,1)} %get-tuple-element.318.h_ref.refs_3_, f32[4,1,2048]{2,1,0:T(1,128)} %reshape.537.lse_ref, s32[4,1,2048]{2,1,0:T(1,128)} %reshape.539.lab_ref), custom_call_target="tpu_custom_call" | custom-call | flops 1000000 | bytes 1000000 | tf_op jit(solution)/shard_map/head_grad/pallas_call | solution.py:469
  555.7 3.1 add_add_fusion.15
  563.6 8.2 fusion.64
  576.0 9.0 shard_map.622.prev
  585.8 25.3 %attn_bwd.2 = (bf16[1024,512]{1,0:T(8,128)(2,1)S(1)}, bf16[1024,512]{1,0:T(8,128)(2,1)S(1)}, bf16[1024,512]{1,0:T(8,128)(2,1)S(1)}, f32[8,512]{1,0:T(8,128)S(1)}) custom-call(f32[8]{0:T(128)S(1)} %pad_maximum_fusion.19.slope_ref, bf16[1024,1536]{1,0:T(8,128)(2,1)} %copy-done.2, bf16[1024,1536]{1,0:T(8,128)(2,1)} %copy-done.2, bf16[1024,1536]{1,0:T(8,128)(2,1)} %copy-done.2, ...), custom_call_target="tpu_custom_call" | custom-call | flops 1000000 | bytes 1000000 | tf_op jit(solution)/shard_map/attn_bwd/pallas_call | solution.py:342
  611.2 3.9 multiply_reduce_fusion.4
  615.1 5.1 shard_map.623
  624.8 79.5 %shard_map.624 = (f32[1,768,256]{2,1,0:T(8,128)}, f32[8,128]{1,0:T(8,128)}, f32[1600,512]{1,0:T(8,128)}) custom-call(f32[8,2,768,256]{3,2,1,0:T(8,128)} %bitcast.268, f32[8,128]{1,0:T(8,128)} %broadcast_12_refs_1__tok_ref.2.refs_1_.tok_ref, bf16[6400,512]{1,0:T(8,128)(2,1)} %copy-done, bf16[8192,512]{1,0:T(8,128)(2,1)} %get-tuple-element.318.h_ref.refs_3_, ...), custom_call_target="tpu_custom_call" | custom-call | flops 1000000 | bytes 1000000 | tf_op jit(solution)/shard_map/pallas_call | solution.py:702
  706.6 9.7 fusion.63
  723.1 25.3 %attn_bwd.3 = (bf16[1024,512]{1,0:T(8,128)(2,1)S(1)}, bf16[1024,512]{1,0:T(8,128)(2,1)S(1)}, bf16[1024,512]{1,0:T(8,128)(2,1)S(1)}, f32[8,512]{1,0:T(8,128)S(1)}) custom-call(f32[8]{0:T(128)S(1)} %pad_maximum_fusion.19.slope_ref, bf16[1024,1536]{1,0:T(8,128)(2,1)} %copy-done.1, bf16[1024,1536]{1,0:T(8,128)(2,1)} %copy-done.1, bf16[1024,1536]{1,0:T(8,128)(2,1)} %copy-done.1, ...), custom_call_target="tpu_custom_call" | custom-call | flops 1000000 | bytes 1000000 | tf_op jit(solution)/shard_map/attn_bwd/pallas_call | solution.py:342
  763.3 9.9 shard_map.625.prev
  777.0 5.1 shard_map.626
  782.7 109.3 %shard_map.627 = (f32[1,768,256]{2,1,0:T(8,128)}, f32[128,128]{1,0:T(8,128)}, f32[1600,512]{1,0:T(8,128)}) custom-call(f32[8,2,768,256]{3,2,1,0:T(8,128)} %bitcast.269, f32[128,128]{1,0:T(8,128)} %maximum_bitcast_fusion.refs_1_, bf16[6400,512]{1,0:T(8,128)(2,1)} %copy-done, bf16[8192,512]{1,0:T(8,128)(2,1)} %get-tuple-element.318.h_ref.refs_3_, ...), custom_call_target="tpu_custom_call" | custom-call | flops 1000000 | bytes 1000000 | tf_op jit(solution)/shard_map/pallas_call | solution.py:702
  894.5 41.6 %all-gather.8.cloned.1.call-done.d_hbm = f32[16384,4,128]{2,1,0:T(4,128)} async-done(((f32[1024,4,128]{2,1,0:T(4,128)}), f32[16384,4,128]{2,1,0:T(4,128)}) %all-gather.8.cloned.1.call-update) | async-done | bytes 33554448 | tf_op jit(solution)/shard_map/all_gather | solution.py:971
  939.3 28.1 %lookup_rows.1 = (f32[3144,256]{1,0:T(8,128)}, f32[3144,256]{1,0:T(8,128)}, f32[8,128]{1,0:T(8,128)}) custom-call(s32[1]{0:T(128)} %bitcast.19.count_ref, s32[16384]{0:T(1024)} %compare_select_fusion.key_ref, f32[16384,4,128]{2,1,0:T(4,128)} %all-gather.8.cloned.1.call-done.d_hbm, f32[1600,512]{1,0:T(8,128)} %get-tuple-element.326.refs_0_, ...), custom_call_target="tpu_custom_call" | custom-call | flops 1000000 | bytes 1000000 | tf_op jit(solution)/shard_map/lookup_rows/pallas_call | solution.py:534
  971.6 7.8 shard_map.628
  984.5 19.0 %adam_rows.12 = (f32[25152,512]{1,0:T(8,128)}, f32[25152,512]{1,0:T(8,128)}, f32[25152,512]{1,0:T(8,128)}, bf16[25152,512]{1,0:T(8,128)(2,1)}, f32[8,128]{1,0:T(8,128)S(1)}) custom-call(s32[2,2]{1,0:T(2,128)S(1)} %get-tuple-element.654.where_ref, f32[1]{0:T(128)} %bitcast.131.clip_ref, f32[8,128]{1,0:T(8,128)S(1)} %copy-done.38, ...), custom_call_target="tpu_custom_call" | custom-call | flops 1000000 | bytes 1000000 | tf_op jit(solution)/shard_map/adam_rows/pallas_call | solution.py:740
  1003.5 18.8 %adam_rows.13 = (f32[25152,512]{1,0:T(8,128)}, f32[25152,512]{1,0:T(8,128)}, f32[25152,512]{1,0:T(8,128)}, bf16[25152,512]{1,0:T(8,128)(2,1)}, f32[8,128]{1,0:T(8,128)S(1)}) custom-call(s32[2,2]{1,0:T(2,128)S(1)} %get-tuple-element.653.where_ref, f32[1]{0:T(128)} %bitcast.131.clip_ref, ...), custom_call_target="tpu_custom_call", output_to_operand_aliasing={{0}: (8, {}), {1}: (9, {}), {2}: (10, {}), {3}: (11, {})} | custom-call | flops 1000000 | bytes 1000000 | tf_op jit(solution)/shard_map/adam_rows/pallas_call | solution.py:740
  1022.2 51.4 %collective-permute-done.36.refs_0_ = f32[3144,256]{1,0:T(8,128)S(1)} collective-permute-done((f32[3144,256]{1,0:T(8,128)}, f32[3144,256]{1,0:T(8,128)S(1)}, u32[]{:S(2)}, u32[]{:S(2)}) %collective-permute-start.36) | collective-permute-done | bytes 3219488 | tf_op jit(solution)/shard_map/ppermute | solution.py:758
  1076.9 17.8 %adam_rows.14 = (f32[25152,512]{1,0:T(8,128)}, f32[25152,512]{1,0:T(8,128)}, f32[25152,512]{1,0:T(8,128)}, bf16[25152,512]{1,0:T(8,128)(2,1)}, f32[8,128]{1,0:T(8,128)S(1)}) custom-call(s32[2,2]{1,0:T(2,128)S(1)} %get-tuple-element.651.where_ref, f32[1]{0:T(128)} %bitcast.131.clip_ref, ...), custom_call_target="tpu_custom_call", output_to_operand_aliasing={{0}: (8, {}), {1}: (9, {}), {2}: (10, {}), {3}: (11, {})} | custom-call | flops 1000000 | bytes 1000000 | tf_op jit(solution)/shard_map/adam_rows/pallas_call | solution.py:740
  1094.8 18.7 %adam_rows.15 = (f32[25152,512]{1,0:T(8,128)}, f32[25152,512]{1,0:T(8,128)}, f32[25152,512]{1,0:T(8,128)}, bf16[25152,512]{1,0:T(8,128)(2,1)}, f32[8,128]{1,0:T(8,128)S(1)}) custom-call(s32[2,2]{1,0:T(2,128)S(1)} %get-tuple-element.655.where_ref, f32[1]{0:T(128)} %bitcast.131.clip_ref, ...), custom_call_target="tpu_custom_call", output_to_operand_aliasing={{0}: (8, {}), {1}: (9, {}), {2}: (10, {}), {3}: (11, {})} | custom-call | flops 1000000 | bytes 1000000 | tf_op jit(solution)/shard_map/adam_rows/pallas_call | solution.py:740
  1113.5 32.7 %collective-permute-done.46.refs_0_ = f32[3144,256]{1,0:T(8,128)} collective-permute-done((f32[3144,256]{1,0:T(8,128)}, f32[3144,256]{1,0:T(8,128)}, u32[]{:S(2)}, u32[]{:S(2)}) %collective-permute-start.46) | collective-permute-done | bytes 3219488 | tf_op jit(solution)/shard_map/ppermute | solution.py:758
  1150.1 3.6 fusion.65
  1155.3 18.7 %adam_rows.16 = (f32[25152,512]{1,0:T(8,128)}, f32[25152,512]{1,0:T(8,128)}, f32[25152,512]{1,0:T(8,128)}, bf16[25152,512]{1,0:T(8,128)(2,1)}, f32[8,128]{1,0:T(8,128)S(1)}) custom-call(s32[2,2]{1,0:T(2,128)S(1)} %get-tuple-element.659.where_ref, f32[1]{0:T(128)} %bitcast.131.clip_ref, ...), custom_call_target="tpu_custom_call", output_to_operand_aliasing={{0}: (8, {}), {1}: (9, {}), {2}: (10, {}), {3}: (11, {})} | custom-call | flops 1000000 | bytes 1000000 | tf_op jit(solution)/shard_map/adam_rows/pallas_call | solution.py:740
  1175.8 18.0 %adam_rows.17 = (f32[25152,512]{1,0:T(8,128)}, f32[25152,512]{1,0:T(8,128)}, f32[25152,512]{1,0:T(8,128)}, bf16[25152,512]{1,0:T(8,128)(2,1)}, f32[8,128]{1,0:T(8,128)S(1)}) custom-call(s32[2,2]{1,0:T(2,128)S(1)} %get-tuple-element.661.where_ref, f32[1]{0:T(128)} %bitcast.131.clip_ref, ...), custom_call_target="tpu_custom_call", output_to_operand_aliasing={{0}: (8, {}), {1}: (9, {}), {2}: (10, {}), {3}: (11, {})} | custom-call | flops 1000000 | bytes 1000000 | tf_op jit(solution)/shard_map/adam_rows/pallas_call | solution.py:740
  1196.5 7.0 adam_rows.18
  1203.6 6.4 adam_rows.19
  1210.0 10.3 collective-permute-done.42.refs_0_
  1225.7 7.1 adam_rows.20
  1233.0 6.4 adam_rows.21
  1239.4 7.6 collective-permute-done.40.refs_0_
  1250.8 7.3 adam_rows.22
  1262.5 6.7 adam_rows.23
  1276.7 32.9 %adam_layers.1 = (f32[2,1024,512]{2,1,0:T(8,128)}, f32[2,512,1024]{2,1,0:T(8,128)}, f32[2,256,512]{2,1,0:T(8,128)}, f32[2,512,768]{2,1,0:T(8,128)}, f32[2,1024,5...) custom-call(f32[1]{0:T(128)} %bitcast.154.clip_ref, ...), custom_call_target="tpu_custom_call" | custom-call | flops 1000000 | bytes 1000000 | tf_op jit(solution)/shard_map/adam_layers/pallas_call | solution.py:201
  (670 shorter events, 212.1 us)
Async XLA Ops:
  7.2 107.7 %all-gather.10.cloned.1.call-start = ((), (), s32[]{:S(2)}) async-start(), calls=%async_computation.1 | async-start | bytes 7077888 | tf_op jit(solution)/shard_map/all_gather | solution.py:787
  9.3 21.0 %collective-permute-start.5 = (f32[768,256]{1,0:T(8,128)}, f32[768,256]{1,0:T(8,128)S(1)}, u32[]{:S(2)}, u32[]{:S(2)}) collective-permute-start(f32[768,256]{1,0:T(8,128)} %pack_share.2), channel_id=1, source_target_pairs={{0,8},{8,0},{1,9},{9,1},{2,10},{10,2},{3,11},{11,3},{4,12},{12,4},... | collective-permute-start | bytes 2359304 | tf_op jit(solution)/shard_map/ppermute | solution.py:758
  31.3 123.0 %all-gather.12.cloned.1.call-start = ((), (), s32[]{:S(2)}) async-start(), calls=%async_computation.2 | async-start | bytes 7077888 | tf_op jit(solution)/shard_map/all_gather | solution.py:787
  33.4 18.9 %collective-permute-start.6 = (f32[768,256]{1,0:T(8,128)}, f32[768,256]{1,0:T(8,128)S(1)}, u32[]{:S(2)}, u32[]{:S(2)}) collective-permute-start(f32[768,256]{1,0:T(8,128)} %pack_share.3), channel_id=1, source_target_pairs={{0,8},{8,0},{1,9},{9,1},{2,10},{10,2},{3,11},{11,3},{4,12},{12,4},... | collective-permute-start | bytes 2359304 | tf_op jit(solution)/shard_map/ppermute | solution.py:758
  53.2 882.9 %all-gather.8.cloned.1.call-start = ((), (), s32[]{:S(2)}) async-start(), calls=%async_computation | async-start | bytes 35651584 | tf_op jit(solution)/shard_map/all_gather | solution.py:971
  53.4 36.5 %collective-permute-start.1 = (s32[2,2,1024]{2,1,0:T(2,128)S(1)}, s32[2,2,1024]{2,1,0:T(2,128)S(1)}, u32[]{:S(2)}, u32[]{:S(2)}) collective-permute-start(s32[2,2,1024]{2,1,0:T(2,128)S(1)} %get-tuple-element.598), channel_id=1, source_target_pairs={{0,1},{1,0},{2,3},{3,2},{4,5},{5,4},{6,7},{7,6},{8,9},{9,8},{10,11... | collective-permute-start | bytes 49160 | tf_op jit(solution)/shard_map/ppermute | solution.py:758
  53.5 61.4 %collective-permute-start.4 = (f32[2,1792]{1,0:T(2,128)S(1)}, f32[2,1792]{1,0:T(2,128)S(1)}, u32[]{:S(2)}, u32[]{:S(2)}) collective-permute-start(f32[2,1792]{1,0:T(2,128)S(1)} %pad_maximum_fusion.6), channel_id=1, source_target_pairs={{0,8},{8,0},{1,9},{9,1},{2,10},{10,2},{3,11},{11,3},{4,12},{12,4},... | collective-permute-start | bytes 43016 | tf_op jit(solution)/shard_map/ppermute | solution.py:758
  63.6 67.3 %collective-permute-start = (f32[1024,512]{1,0:T(8,128)}, f32[1024,512]{1,0:T(8,128)}, u32[]{:S(2)}, u32[]{:S(2)}) collective-permute-start(f32[1024,512]{1,0:T(8,128)} %broadcast_select_fusion.3), channel_id=1, source_target_pairs={{0,8},{8,0},{1,9},{9,1},{2,10},{10,2},{3,11},{11,3},{4,12},{12,4},... | collective-permute-start | bytes 6291464 | tf_op jit(solution)/shard_map/ppermute | solution.py:758
  89.9 10.6 collective-permute-start.2
  100.5 6.2 collective-permute-start.3
  213.3 4.3 collective-permute-start.7
  218.7 26.3 %collective-permute-start.8 = (f32[512,512]{1,0:T(8,128)}, f32[512,512]{1,0:T(8,128)}, u32[]{:S(2)}, u32[]{:S(2)}) collective-permute-start(f32[512,512]{1,0:T(8,128)} %get-tuple-element.254), channel_id=1, source_target_pairs={{0,2},{1,3},{2,0},{3,1},{4,6},{5,7},{6,4},{7,5},{8,10},{9,11},{10,... | collective-permute-start | bytes 3145736 | tf_op jit(solution)/shard_map/ppermute | solution.py:758
  219.7 26.4 %collective-permute-start.9 = (f32[512,512]{1,0:T(8,128)}, f32[512,512]{1,0:T(8,128)}, u32[]{:S(2)}, u32[]{:S(2)}) collective-permute-start(f32[512,512]{1,0:T(8,128)} %get-tuple-element.254), channel_id=1, source_target_pairs={{0,8},{8,0},{1,9},{9,1},{2,10},{10,2},{3,11},{11,3},{4,12},{12,4},... | collective-permute-start | bytes 3145736 | tf_op jit(solution)/shard_map/ppermute | solution.py:758
  221.2 62.3 %collective-permute-start.12 = (f32[512,512]{1,0:T(8,128)S(1)}, f32[512,512]{1,0:T(8,128)S(1)}, u32[]{:S(2)}, u32[]{:S(2)}) collective-permute-start(f32[512,512]{1,0:T(8,128)S(1)} %get-tuple-element.255), channel_id=1, source_target_pairs={{0,2},{1,3},{2,0},{3,1},{4,6},{5,7},{6,4},{7,5},{8,10},{9,11},{10,... | collective-permute-start | bytes 3145736 | tf_op jit(solution)/shard_map/ppermute | solution.py:758
  222.4 61.1 %collective-permute-start.13 = (f32[512,512]{1,0:T(8,128)S(1)}, f32[512,512]{1,0:T(8,128)S(1)}, u32[]{:S(2)}, u32[]{:S(2)}) collective-permute-start(f32[512,512]{1,0:T(8,128)S(1)} %get-tuple-element.255), channel_id=1, source_target_pairs={{0,8},{8,0},{1,9},{9,1},{2,10},{10,2},{3,11},{11,3},{4,12},{12,4},... | collective-permute-start | bytes 3145736 | tf_op jit(solution)/shard_map/ppermute | solution.py:758
  246.0 40.7 %collective-permute-start.14 = (f32[512,512]{1,0:T(8,128)}, f32[512,512]{1,0:T(8,128)}, u32[]{:S(2)}, u32[]{:S(2)}) collective-permute-start(f32[512,512]{1,0:T(8,128)} %collective-permute-done.8.refs_1_), channel_id=1, source_target_pairs={{0,1},{1,0},{2,3},{3,2},{4,5},{5,4},{6,7},{7,6},{8,9},{9,8},{10,11... | collective-permute-start | bytes 3145736 | tf_op jit(solution)/shard_map/ppermute | solution.py:758
  283.5 50.4 %collective-permute-start.18 = (f32[512,512]{1,0:T(8,128)S(1)}, f32[512,512]{1,0:T(8,128)}, u32[]{:S(2)}, u32[]{:S(2)}) collective-permute-start(f32[512,512]{1,0:T(8,128)S(1)} %collective-permute-done.12.refs_1_), channel_id=1, source_target_pairs={{0,1},{1,0},{2,3},{3,2},{4,5},{5,4},{6,7},{7,6},{8,9},{9,8},{10,11... | collective-permute-start | bytes 3145736 | tf_op jit(solution)/shard_map/ppermute | solution.py:758
  284.1 49.8 %collective-permute-start.19 = (f32[512,512]{1,0:T(8,128)S(1)}, f32[512,512]{1,0:T(8,128)}, u32[]{:S(2)}, u32[]{:S(2)}) collective-permute-start(f32[512,512]{1,0:T(8,128)S(1)} %collective-permute-done.13.refs_2_), channel_id=1, source_target_pairs={{0,1},{1,0},{2,3},{3,2},{4,5},{5,4},{6,7},{7,6},{8,9},{9,8},{10,11... | collective-permute-start | bytes 3145736 | tf_op jit(solution)/shard_map/ppermute | solution.py:758
  284.1 5.6 collective-permute-start.15
  284.6 42.5 %collective-permute-start.10 = (f32[512,512]{1,0:T(8,128)}, f32[512,512]{1,0:T(8,128)S(1)}, u32[]{:S(2)}, u32[]{:S(2)}) collective-permute-start(f32[512,512]{1,0:T(8,128)} %get-tuple-element.254), channel_id=1, source_target_pairs={{0,10},{1,11},{2,8},{3,9},{4,14},{5,15},{6,12},{7,13},{8,2},{9,3},... | collective-permute-start | bytes 3145736 | tf_op jit(solution)/shard_map/ppermute | solution.py:757
  286.7 46.6 %collective-permute-start.11 = (f32[512,512]{1,0:T(8,128)}, f32[512,512]{1,0:T(8,128)}, u32[]{:S(2)}, u32[]{:S(2)}) collective-permute-start(f32[512,512]{1,0:T(8,128)} %copy-done.90), channel_id=1, source_target_pairs={{0,10},{1,11},{2,8},{3,9},{4,14},{5,15},{6,12},{7,13},{8,2},{9,3},... | collective-permute-start | bytes 3145736 | tf_op jit(solution)/shard_map/ppermute | solution.py:757
  289.7 117.0 %collective-permute-start.23 = (f32[1024,512]{1,0:T(8,128)}, f32[1024,512]{1,0:T(8,128)}, u32[]{:S(2)}, u32[]{:S(2)}) collective-permute-start(f32[1024,512]{1,0:T(8,128)} %get-tuple-element.280), channel_id=1, source_target_pairs={{0,1},{1,0},{2,3},{3,2},{4,5},{5,4},{6,7},{7,6},{8,9},{9,8},{10,11... | collective-permute-start | bytes 6291464 | tf_op jit(solution)/shard_map/ppermute | solution.py:758
  333.4 40.5 %collective-permute-start.16 = (f32[512,512]{1,0:T(8,128)S(1)}, f32[512,512]{1,0:T(8,128)}, u32[]{:S(2)}, u32[]{:S(2)}) collective-permute-start(f32[512,512]{1,0:T(8,128)S(1)} %collective-permute-done.10.refs_1_), channel_id=1, source_target_pairs={{0,1},{1,0},{2,3},{3,2},{4,5},{5,4},{6,7},{7,6},{8,9},{9,8},{10,11... | collective-permute-start | bytes 3145736 | tf_op jit(solution)/shard_map/ppermute | solution.py:758
  333.4 40.5 %collective-permute-start.17 = (f32[512,512]{1,0:T(8,128)}, f32[512,512]{1,0:T(8,128)}, u32[]{:S(2)}, u32[]{:S(2)}) collective-permute-start(f32[512,512]{1,0:T(8,128)} %collective-permute-done.11.refs_2_), channel_id=1, source_target_pairs={{0,1},{1,0},{2,3},{3,2},{4,5},{5,4},{6,7},{7,6},{8,9},{9,8},{10,11... | collective-permute-start | bytes 3145736 | tf_op jit(solution)/shard_map/ppermute | solution.py:758
  371.2 39.6 %collective-permute-start.25 = (f32[1024,512]{1,0:T(8,128)}, f32[1024,512]{1,0:T(8,128)}, u32[]{:S(2)}, u32[]{:S(2)}) collective-permute-start(f32[1024,512]{1,0:T(8,128)} %get-tuple-element.284), channel_id=1, source_target_pairs={{0,1},{1,0},{2,3},{3,2},{4,5},{5,4},{6,7},{7,6},{8,9},{9,8},{10,11... | collective-permute-start | bytes 6291464 | tf_op jit(solution)/shard_map/ppermute | solution.py:758
  371.2 41.8 %collective-permute-start.24 = (f32[1024,512]{1,0:T(8,128)}, f32[1024,512]{1,0:T(8,128)}, u32[]{:S(2)}, u32[]{:S(2)}) collective-permute-start(f32[1024,512]{1,0:T(8,128)} %get-tuple-element.282), channel_id=1, source_target_pairs={{0,1},{1,0},{2,3},{3,2},{4,5},{5,4},{6,7},{7,6},{8,9},{9,8},{10,11... | collective-permute-start | bytes 6291464 | tf_op jit(solution)/shard_map/ppermute | solution.py:758
  396.1 1.3 collective-permute-start.20
  396.1 19.6 %collective-permute-start.26 = (f32[1024,512]{1,0:T(8,128)}, f32[1024,512]{1,0:T(8,128)}, u32[]{:S(2)}, u32[]{:S(2)}) collective-permute-start(f32[1024,512]{1,0:T(8,128)} %get-tuple-element.286), channel_id=1, source_target_pairs={{0,1},{1,0},{2,3},{3,2},{4,5},{5,4},{6,7},{7,6},{8,9},{9,8},{10,11... | collective-permute-start | bytes 6291464 | tf_op jit(solution)/shard_map/ppermute | solution.py:758
  397.5 4.3 collective-permute-start.21
  401.9 4.3 collective-permute-start.22
  420.0 44.0 %collective-permute-start.28 = (f32[512,512]{1,0:T(8,128)}, f32[512,512]{1,0:T(8,128)S(1)}, u32[]{:S(2)}, u32[]{:S(2)}) collective-permute-start(f32[512,512]{1,0:T(8,128)} %get-tuple-element.508), channel_id=1, source_target_pairs={{0,8},{8,0},{1,9},{9,1},{2,10},{10,2},{3,11},{11,3},{4,12},{12,4},... | collective-permute-start | bytes 3145736 | tf_op jit(solution)/shard_map/ppermute | solution.py:758
  421.5 42.4 %collective-permute-start.30 = (f32[512,512]{1,0:T(8,128)}, f32[512,512]{1,0:T(8,128)}, u32[]{:S(2)}, u32[]{:S(2)}) collective-permute-start(f32[512,512]{1,0:T(8,128)} %get-tuple-element.507), channel_id=1, source_target_pairs={{0,2},{1,3},{2,0},{3,1},{4,6},{5,7},{6,4},{7,5},{8,10},{9,11},{10,... | collective-permute-start | bytes 3145736 | tf_op jit(solution)/shard_map/ppermute | solution.py:758
  423.8 45.0 %collective-permute-start.27 = (f32[512,512]{1,0:T(8,128)}, f32[512,512]{1,0:T(8,128)}, u32[]{:S(2)}, u32[]{:S(2)}) collective-permute-start(f32[512,512]{1,0:T(8,128)} %slice.785), channel_id=1, source_target_pairs={{0,8},{8,0},{1,9},{9,1},{2,10},{10,2},{3,11},{11,3},{4,12},{12,4},... | collective-permute-start | bytes 3145736 | tf_op jit(solution)/shard_map/ppermute | solution.py:758
  425.2 43.6 %collective-permute-start.29 = (f32[512,512]{1,0:T(8,128)}, f32[512,512]{1,0:T(8,128)}, u32[]{:S(2)}, u32[]{:S(2)}) collective-permute-start(f32[512,512]{1,0:T(8,128)} %slice.787), channel_id=1, source_target_pairs={{0,2},{1,3},{2,0},{3,1},{4,6},{5,7},{6,4},{7,5},{8,10},{9,11},{10,... | collective-permute-start | bytes 3145736 | tf_op jit(solution)/shard_map/ppermute | solution.py:758
  426.2 87.5 %collective-permute-start.33 = (f32[1024,512]{1,0:T(8,128)}, f32[1024,512]{1,0:T(8,128)}, u32[]{:S(2)}, u32[]{:S(2)}) collective-permute-start(f32[1024,512]{1,0:T(8,128)} %broadcast_select_fusion.1), channel_id=1, source_target_pairs={{0,8},{8,0},{1,9},{9,1},{2,10},{10,2},{3,11},{11,3},{4,12},{12,4},... | collective-permute-start | bytes 6291464 | tf_op jit(solution)/shard_map/ppermute | solution.py:758
  472.4 82.4 %collective-permute-start.31 = (f32[512,512]{1,0:T(8,128)}, f32[512,512]{1,0:T(8,128)S(1)}, u32[]{:S(2)}, u32[]{:S(2)}) collective-permute-start(f32[512,512]{1,0:T(8,128)} %slice_add_fusion.1), channel_id=1, source_target_pairs={{0,2},{1,3},{2,0},{3,1},{4,6},{5,7},{6,4},{7,5},{8,10},{9,11},{10,... | collective-permute-start | bytes 3145736 | tf_op jit(solution)/shard_map/ppermute | solution.py:758
  473.5 82.2 %collective-permute-start.32 = (f32[512,512]{1,0:T(8,128)}, f32[512,512]{1,0:T(8,128)}, u32[]{:S(2)}, u32[]{:S(2)}) collective-permute-start(f32[512,512]{1,0:T(8,128)} %slice_add_fusion), channel_id=1, source_target_pairs={{0,8},{8,0},{1,9},{9,1},{2,10},{10,2},{3,11},{11,3},{4,12},{12,4},... | collective-permute-start | bytes 3145736 | tf_op jit(solution)/shard_map/ppermute | solution.py:758
  518.4 92.7 %collective-permute-start.34 = (f32[1600,512]{1,0:T(8,128)}, f32[1600,512]{1,0:T(8,128)}, u32[]{:S(2)}, u32[]{:S(2)}) collective-permute-start(f32[1600,512]{1,0:T(8,128)} %head_grad.2), channel_id=1, source_target_pairs={{0,4},{1,5},{2,6},{3,7},{4,0},{5,1},{6,2},{7,3},{8,12},{9,13},{10,... | collective-permute-start | bytes 9830408 | tf_op jit(solution)/shard_map/ppermute | solution.py:758
  554.0 194.4 %collective-permute-start.35 = (f32[1600,512]{1,0:T(8,128)}, f32[1600,512]{1,0:T(8,128)}, u32[]{:S(2)}, u32[]{:S(2)}) collective-permute-start(f32[1600,512]{1,0:T(8,128)} %head_grad.3), channel_id=1, source_target_pairs={{0,4},{1,5},{2,6},{3,7},{4,0},{5,1},{6,2},{7,3},{8,12},{9,13},{10,... | collective-permute-start | bytes 9830408 | tf_op jit(solution)/shard_map/ppermute | solution.py:758
  759.1 510.1 %all-gather.14.cloned.1.call-start = ((), (), s32[]{:S(2)}) async-start(), calls=%async_computation.3 | async-start | bytes 14155776 | tf_op jit(solution)/shard_map/all_gather | solution.py:1000
  782.7 109.3 %copy-start.94 = (f32[1,768,256]{2,1,0:T(8,128)S(1)}, f32[1,768,256]{2,1,0:T(8,128)}, u32[]{:S(2)}) copy-start(f32[1,768,256]{2,1,0:T(8,128)} %get-tuple-element.324) | copy-start | bytes 2359300
  981.4 22.0 %collective-permute-start.38 = (f32[3144,256]{1,0:T(8,128)}, f32[3144,256]{1,0:T(8,128)}, u32[]{:S(2)}, u32[]{:S(2)}) collective-permute-start(f32[3144,256]{1,0:T(8,128)} %get-tuple-element.335.refs_0_), channel_id=1, source_target_pairs={{0,1},{1,0},{2,3},{3,2},{4,5},{5,4},{6,7},{7,6},{8,9},{9,8},{10,11... | collective-permute-start | bytes 9658376 | tf_op jit(solution)/shard_map/ppermute | solution.py:758
  981.6 21.9 %collective-permute-start.39 = (f32[3144,256]{1,0:T(8,128)}, f32[3144,256]{1,0:T(8,128)}, u32[]{:S(2)}, u32[]{:S(2)}) collective-permute-start(f32[3144,256]{1,0:T(8,128)} %get-tuple-element.336.refs_1_), channel_id=1, source_target_pairs={{0,1},{1,0},{2,3},{3,2},{4,5},{5,4},{6,7},{7,6},{8,9},{9,8},{10,11... | collective-permute-start | bytes 9658376 | tf_op jit(solution)/shard_map/ppermute | solution.py:758
  982.0 91.7 %collective-permute-start.36 = (f32[3144,256]{1,0:T(8,128)}, f32[3144,256]{1,0:T(8,128)S(1)}, u32[]{:S(2)}, u32[]{:S(2)}) collective-permute-start(f32[3144,256]{1,0:T(8,128)} %get-tuple-element.335.refs_0_), channel_id=1, source_target_pairs={{0,2},{1,3},{2,0},{3,1},{4,6},{5,7},{6,4},{7,5},{8,10},{9,11},{10,... | collective-permute-start | bytes 9658376 | tf_op jit(solution)/shard_map/ppermute | solution.py:758
  982.8 90.9 %collective-permute-start.37 = (f32[3144,256]{1,0:T(8,128)}, f32[3144,256]{1,0:T(8,128)}, u32[]{:S(2)}, u32[]{:S(2)}) collective-permute-start(f32[3144,256]{1,0:T(8,128)} %get-tuple-element.336.refs_1_), channel_id=1, source_target_pairs={{0,4},{1,5},{2,6},{3,7},{4,0},{5,1},{6,2},{7,3},{8,12},{9,13},{10,... | collective-permute-start | bytes 9658376 | tf_op jit(solution)/shard_map/ppermute | solution.py:758
  984.5 92.4 %copy-start.145 = (s32[1,2]{1,0:T(1,128)}, s32[1,2]{1,0:T(1,128)S(1)}, u32[]{:S(2)}) copy-start(s32[1,2]{1,0:T(1,128)S(1)} %iota.5) | copy-start | bytes 28
  1073.7 21.0 %collective-permute-start.48 = (f32[3144,256]{1,0:T(8,128)S(1)}, f32[3144,256]{1,0:T(8,128)}, u32[]{:S(2)}, u32[]{:S(2)}) collective-permute-start(f32[3144,256]{1,0:T(8,128)S(1)} %collective-permute-done.36.refs_0_), channel_id=1, source_target_pairs={{0,1},{1,0},{2,3},{3,2},{4,5},{5,4},{6,7},{7,6},{8,9},{9,8},{10,11... | collective-permute-start | bytes 9658376 | tf_op jit(solution)/shard_map/ppermute | solution.py:758
  1073.7 21.1 %collective-permute-start.49 = (f32[3144,256]{1,0:T(8,128)}, f32[3144,256]{1,0:T(8,128)}, u32[]{:S(2)}, u32[]{:S(2)}) collective-permute-start(f32[3144,256]{1,0:T(8,128)} %collective-permute-done.37.refs_1_), channel_id=1, source_target_pairs={{0,1},{1,0},{2,3},{3,2},{4,5},{5,4},{6,7},{7,6},{8,9},{9,8},{10,11... | collective-permute-start | bytes 9658376 | tf_op jit(solution)/shard_map/ppermute | solution.py:758
  1074.2 71.9 %collective-permute-start.46 = (f32[3144,256]{1,0:T(8,128)}, f32[3144,256]{1,0:T(8,128)}, u32[]{:S(2)}, u32[]{:S(2)}) collective-permute-start(f32[3144,256]{1,0:T(8,128)} %get-tuple-element.335.refs_0_), channel_id=1, source_target_pairs={{0,4},{1,5},{2,6},{3,7},{4,0},{5,1},{6,2},{7,3},{8,12},{9,13},{10,... | collective-permute-start | bytes 9658376 | tf_op jit(solution)/shard_map/ppermute | solution.py:758
  1075.6 71.6 %collective-permute-start.47 = (f32[3144,256]{1,0:T(8,128)}, f32[3144,256]{1,0:T(8,128)}, u32[]{:S(2)}, u32[]{:S(2)}) collective-permute-start(f32[3144,256]{1,0:T(8,128)} %get-tuple-element.336.refs_1_), channel_id=1, source_target_pairs={{0,2},{1,3},{2,0},{3,1},{4,6},{5,7},{6,4},{7,5},{8,10},{9,11},{10,... | collective-permute-start | bytes 9658376 | tf_op jit(solution)/shard_map/ppermute | solution.py:758
  1147.2 26.8 %collective-permute-start.50 = (f32[3144,256]{1,0:T(8,128)}, f32[3144,256]{1,0:T(8,128)S(1)}, u32[]{:S(2)}, u32[]{:S(2)}) collective-permute-start(f32[3144,256]{1,0:T(8,128)} %collective-permute-done.46.refs_0_), channel_id=1, source_target_pairs={{0,1},{1,0},{2,3},{3,2},{4,5},{5,4},{6,7},{7,6},{8,9},{9,8},{10,11... | collective-permute-start | bytes 9658376 | tf_op jit(solution)/shard_map/ppermute | solution.py:758
  1147.2 26.8 %collective-permute-start.51 = (f32[3144,256]{1,0:T(8,128)}, f32[3144,256]{1,0:T(8,128)S(1)}, u32[]{:S(2)}, u32[]{:S(2)}) collective-permute-start(f32[3144,256]{1,0:T(8,128)} %collective-permute-done.47.refs_1_), channel_id=1, source_target_pairs={{0,1},{1,0},{2,3},{3,2},{4,5},{5,4},{6,7},{7,6},{8,9},{9,8},{10,11... | collective-permute-start | bytes 9658376 | tf_op jit(solution)/shard_map/ppermute | solution.py:758
  1149.5 44.3 %collective-permute-start.44 = (f32[1048,256]{1,0:T(8,128)}, f32[1048,256]{1,0:T(8,128)}, u32[]{:S(2)}, u32[]{:S(2)}) collective-permute-start(f32[1048,256]{1,0:T(8,128)} %get-tuple-element.498), channel_id=1, source_target_pairs={{0,4},{1,5},{2,6},{3,7},{4,0},{5,1},{6,2},{7,3},{8,12},{9,13},{10,... | collective-permute-start | bytes 3219464 | tf_op jit(solution)/shard_map/ppermute | solution.py:758
  1153.8 40.0 %collective-permute-start.45 = (f32[1048,256]{1,0:T(8,128)}, f32[1048,256]{1,0:T(8,128)}, u32[]{:S(2)}, u32[]{:S(2)}) collective-permute-start(f32[1048,256]{1,0:T(8,128)} %get-tuple-element.495), channel_id=1, source_target_pairs={{0,2},{1,3},{2,0},{3,1},{4,6},{5,7},{6,4},{7,5},{8,10},{9,11},{10,... | collective-permute-start | bytes 3219464 | tf_op jit(solution)/shard_map/ppermute | solution.py:758
  1193.8 9.7 collective-permute-start.52
  1193.9 9.7 collective-permute-start.53
  1194.4 26.0 %collective-permute-start.42 = (f32[1048,256]{1,0:T(8,128)}, f32[1048,256]{1,0:T(8,128)}, u32[]{:S(2)}, u32[]{:S(2)}) collective-permute-start(f32[1048,256]{1,0:T(8,128)} %get-tuple-element.499), channel_id=1, source_target_pairs={{0,4},{1,5},{2,6},{3,7},{4,0},{5,1},{6,2},{7,3},{8,12},{9,13},{10,... | collective-permute-start | bytes 3219464 | tf_op jit(solution)/shard_map/ppermute | solution.py:758
  1194.9 25.7 %collective-permute-start.43 = (f32[1048,256]{1,0:T(8,128)}, f32[1048,256]{1,0:T(8,128)}, u32[]{:S(2)}, u32[]{:S(2)}) collective-permute-start(f32[1048,256]{1,0:T(8,128)} %get-tuple-element.496), channel_id=1, source_target_pairs={{0,2},{1,3},{2,0},{3,1},{4,6},{5,7},{6,4},{7,5},{8,10},{9,11},{10,... | collective-permute-start | bytes 3219464 | tf_op jit(solution)/shard_map/ppermute | solution.py:758
  1220.6 12.2 collective-permute-start.54
  1220.6 12.2 collective-permute-start.55
  1221.1 25.9 %collective-permute-start.40 = (f32[1048,256]{1,0:T(8,128)}, f32[1048,256]{1,0:T(8,128)}, u32[]{:S(2)}, u32[]{:S(2)}) collective-permute-start(f32[1048,256]{1,0:T(8,128)} %get-tuple-element.500), channel_id=1, source_target_pairs={{0,4},{1,5},{2,6},{3,7},{4,0},{5,1},{6,2},{7,3},{8,12},{9,13},{10,... | collective-permute-start | bytes 3219464 | tf_op jit(solution)/shard_map/ppermute | solution.py:758
  1222.6 25.6 %collective-permute-start.41 = (f32[1048,256]{1,0:T(8,128)}, f32[1048,256]{1,0:T(8,128)}, u32[]{:S(2)}, u32[]{:S(2)}) collective-permute-start(f32[1048,256]{1,0:T(8,128)} %get-tuple-element.497), channel_id=1, source_target_pairs={{0,2},{1,3},{2,0},{3,1},{4,6},{5,7},{6,4},{7,5},{8,10},{9,11},{10,... | collective-permute-start | bytes 3219464 | tf_op jit(solution)/shard_map/ppermute | solution.py:758
  1248.2 9.9 collective-permute-start.56
  1248.2 10.9 collective-permute-start.57
  (151 other events, 1703.7 us)
Sparse Core Ops, SparseCore 0:
  31.4 42.8 all-gather.9
  76.7 43.2 all-gather.11
  759.3 176.8 all-gather.7
  938.4 87.5 all-gather.13
